TPU v7x, 128 devices: a whole 4x4x4 slice. The times are simulated.
128 devices in a mesh: band: 64 (over y, z, x_hi, core), grid: 2 (over x_lo).
Axes of the slice: x: 4 (x_hi: 2, x_lo: 2; x = x_hi * 2 + x_lo), y: 4, z: 4, core: 2. Of those that a mesh axis runs over, the one named last changes fastest.
Arguments:
- bands: float32 [128, 72, 5184], P('band', 'grid'), may hold values from -2.4 to 2.4
Outputs:
- exchange_terms: float32 [128, 72, 5184], P('band', 'grid')
All inputs are finite; a program needn't handle non-finite values.
Results may differ from a plain program's by a relative error of at most 0.0001.
Values sent between devices are 32-bit elements; how exact they have to be, the bound alone decides.
A program may use at most 128 MiB of HBM per device.

v0:
```python
import math

import jax
import jax.numpy as jnp
from jax import lax
from jax.sharding import PartitionSpec as P

GRID = 72
STEPS = 3


spacing = 0.5167


def shifted(value, axis, steps):
    count = lax.axis_size(axis)
    pairs = [(source, (source + steps) % count) for source in range(count)]
    return lax.ppermute(value, axis, pairs)


def split_up(array, dim, devices):
    before, after = (array.shape[:dim], array.shape[dim + 1 :])
    return jnp.moveaxis(array.reshape(*before, devices, -1, *after), dim, 0)


def sent_and_summed(array, axis, dim):
    devices = lax.axis_size(axis)
    blocks = lax.all_to_all(split_up(array, dim, devices), axis, 0, 0, tiled=True)
    return jnp.sum(blocks, axis=0)


def tables(count):
    index = jnp.arange(count, dtype=jnp.int32)
    half = count // 2
    freq = jnp.where(index <= half, index, index - half)
    phase = (freq[:, None] * index[None, :] % count).astype(jnp.float32) * (2.0 * math.pi / count)
    table = jnp.where(index[:, None] <= half, jnp.cos(phase), jnp.sin(phase))
    weight = jnp.where((index == 0) | (index == half), 1.0, 2.0).astype(jnp.float32)
    square = freq.astype(jnp.float32) ** 2
    factor = (2.0 * math.pi / (count * spacing)) ** 2
    ksq = factor * (square[:, None, None] + square[None, :, None] + square[None, None, :])
    safe = jnp.where(ksq > 0, ksq, 1.0)
    coulomb = jnp.where(ksq > 0, 4.0 * math.pi / safe, 0.0)
    weights = weight[:, None, None] * weight[None, :, None] * weight[None, None, :]
    kernel = coulomb * weights / float(count**3)
    return (table, kernel.reshape(count, count * count))


def forward_axis(values, table):
    return jnp.einsum("pmc,kc->pkm", values, table, precision=lax.Precision.HIGHEST)


def inverse_axis(values, table):
    return jnp.einsum("pmk,kr->prm", values, table, precision=lax.Precision.HIGHEST)


def coulomb_filter(density, table, kernel):
    count = table.shape[0]
    pairs = density.shape[0]
    work = forward_axis(density.reshape(pairs, count * count, count), table)
    work = forward_axis(work.reshape(pairs, count * count, count), table)
    work = forward_axis(work.reshape(pairs, count * count, count), table)
    work = work * kernel[None]
    work = inverse_axis(work.reshape(pairs, count * count, count), table)
    work = inverse_axis(work.reshape(pairs, count * count, count), table)
    work = inverse_axis(work.reshape(pairs, count * count, count), table)
    return work


def pair_terms(home, visit, table, kernel):
    home_count = home.shape[0]
    visit_count = visit.shape[0]
    count = home.shape[1]
    density = (home[:, None] * visit[None]).reshape(home_count * visit_count, count, home.shape[2])
    potential = coulomb_filter(density, table, kernel).reshape(
        home_count, visit_count, count, home.shape[2]
    )
    home_part = -jnp.sum(potential * visit[None], axis=1)
    partner = -jnp.sum(potential * home[:, None], axis=0)
    return (home_part, partner)


def local(bands):
    table, kernel = tables(GRID)
    whole = lax.all_gather(bands, "grid", axis=1, tiled=True)
    share = whole.shape[0] // lax.axis_size("grid")
    first = lax.axis_index("grid") * share
    visit = lax.dynamic_slice_in_dim(whole, first, share, 0)
    home_total = jnp.zeros_like(whole)
    carried = jnp.zeros_like(visit)
    for step in range(STEPS):
        visit = shifted(visit, "band", 1)
        home_part, partner = pair_terms(whole, visit, table, kernel)
        home_total = home_total + home_part
        carried = carried + partner
        if step + 1 < STEPS:
            carried = shifted(carried, "band", 1)
    returned = shifted(carried, "band", -STEPS)
    own_rows = lax.dynamic_slice_in_dim(home_total, first, share, 0) + returned
    home_total = lax.dynamic_update_slice_in_dim(home_total, own_rows, first, 0)
    return sent_and_summed(home_total, "grid", 1)


def solution(mesh):
    return jax.shard_map(
        local,
        mesh=mesh,
        in_specs=(P("band", "grid", None),),
        out_specs=P("band", "grid", None),
        check_vma=False,
    )
```

profile of v0, /device:TPU:4, one launch (start us, length us, event | category | flops | bytes accessed | tf_op | source)
XLA Modules:
  0.0 540.8 jit_solution(13337431884350394181)
XLA Ops:
  7.3 49.8 %all-gather.2.cloned.1.call-done = f32[2,72,5184]{2,0,1:T(2,128)} async-done(((f32[2,36,5184]{2,0,1:T(2,128)}), f32[2,72,5184]{2,0,1:T(2,128)}) %all-gather.2.cloned.1.call-update) | async-done | bytes 2986000 | tf_op jit(solution)/shard_map/all_gather | solution.py:85
  57.1 3.1 constant_dynamic-slice_fusion
  60.3 20.7 %collective-permute-done = f32[1,72,5184]{2,0,1:T(1,128)S(1)} collective-permute-done((f32[1,72,5184]{2,0,1:T(1,128)S(1)}, f32[1,72,5184]{2,0,1:T(1,128)S(1)}, u32[]{:S(2)}, u32[]{:S(2)}) %collective-permute-start) | collective-permute-done | bytes 1493024 | tf_op jit(solution)/shard_map/ppermute | solution.py:18
  82.3 20.6 %collective-permute-done.1 = f32[1,72,5184]{2,0,1:T(1,128)} collective-permute-done((f32[1,72,5184]{2,0,1:T(1,128)S(1)}, f32[1,72,5184]{2,0,1:T(1,128)}, u32[]{:S(2)}, u32[]{:S(2)}) %collective-permute-start.1) | collective-permute-done | bytes 1493024 | tf_op jit(solution)/shard_map/ppermute | solution.py:18
  113.3 10.6 %collective-permute-done.2 = f32[1,72,5184]{2,0,1:T(1,128)} collective-permute-done((f32[1,72,5184]{2,0,1:T(1,128)}, f32[1,72,5184]{2,0,1:T(1,128)}, u32[]{:S(2)}, u32[]{:S(2)}) %collective-permute-start.2) | collective-permute-done | bytes 1493024 | tf_op jit(solution)/shard_map/ppermute | solution.py:18
  125.4 4.1 copy_multiply_fusion.2
  129.5 6.4 %reshape_reshape.9 = f32[2,5184,72]{2,1,0:T(8,128)} reshape(f32[2,72,5184]{2,1,0:T(8,128)} %get-tuple-element.9) | data formatting | bytes 5971968 | tf_op jit(solution)/shard_map/reshape;reshape | solution.py:60
  135.9 9.4 %convolution_bitcast_fusion.14 = f32[2,72,5184]{2,1,0:T(8,128)} fusion(f32[2,5184,72]{2,1,0:T(8,128)} %reshape_reshape.9, s32[72]{0:T(128)S(1)} %add_select_fusion.1, pred[72]{0:T(512)(128)(4,1)S(1)} %iota_compare_fusion), kind=kOutput, calls=%fused_computation.20 | convolution fusion | flops 645024384 | bytes 5972328 | tf_op jit(solution)/shard_map/pmc,kc->pkm/dot_general | solution.py:50
  145.3 5.8 %reshape.283 = f32[2,5184,72]{2,1,0:T(8,128)} reshape(f32[2,72,5184]{2,1,0:T(8,128)} %convolution_bitcast_fusion.14) | data formatting | bytes 5971968 | tf_op jit(solution)/shard_map/reshape | solution.py:61
  151.1 9.4 %convolution_bitcast_fusion.13 = f32[2,72,5184]{2,1,0:T(8,128)} fusion(f32[2,5184,72]{2,1,0:T(8,128)} %reshape.283, s32[72]{0:T(128)S(1)} %add_select_fusion.1, pred[72]{0:T(512)(128)(4,1)S(1)} %iota_compare_fusion), kind=kOutput, calls=%fused_computation.19 | convolution fusion | flops 645024384 | bytes 5972328 | tf_op jit(solution)/shard_map/pmc,kc->pkm/dot_general | solution.py:50
  160.6 6.0 %reshape.284 = f32[2,5184,72]{2,1,0:T(8,128)} reshape(f32[2,72,5184]{2,1,0:T(8,128)} %convolution_bitcast_fusion.13) | data formatting | bytes 5971968 | tf_op jit(solution)/shard_map/reshape | solution.py:62
  166.6 9.4 %fusion = f32[2,72,5184]{2,1,0:T(8,128)} fusion(f32[2,5184,72]{2,1,0:T(8,128)} %reshape.284, f32[72,5184]{1,0:T(8,128)S(1)} %fusion.5, s32[72]{0:T(128)S(1)} %add_select_fusion.1, pred[72]{0:T(512)(128)(4,1)S(1)} %iota_compare_fusion), kind=kOutput, calls=%fused_computation.3 | convolution fusion | flops 645770880 | bytes 7465320 | tf_op jit(solution)/shard_map/pmc,kc->pkm/dot_general | solution.py:50
  176.0 5.8 %reshape.285 = f32[2,5184,72]{2,1,0:T(8,128)} reshape(f32[2,72,5184]{2,1,0:T(8,128)} %fusion) | data formatting | bytes 5971968 | tf_op jit(solution)/shard_map/reshape | solution.py:64
  181.8 9.7 %convolution_bitcast_fusion.12 = f32[2,72,5184]{2,1,0:T(8,128)} fusion(f32[2,5184,72]{2,1,0:T(8,128)} %reshape.285, s32[72]{0:T(128)S(1)} %add_select_fusion.1, pred[72]{0:T(512)(128)(4,1)S(1)} %iota_compare_fusion), kind=kOutput, calls=%fused_computation.18 | convolution fusion | flops 645024384 | bytes 5972328 | tf_op jit(solution)/shard_map/pmk,kr->prm/dot_general | solution.py:54
  191.5 6.0 %reshape.286 = f32[2,5184,72]{2,1,0:T(8,128)} reshape(f32[2,72,5184]{2,1,0:T(8,128)} %convolution_bitcast_fusion.12) | data formatting | bytes 5971968 | tf_op jit(solution)/shard_map/reshape | solution.py:65
  197.6 9.7 %convolution_bitcast_fusion.11 = f32[2,72,5184]{2,1,0:T(8,128)} fusion(f32[2,5184,72]{2,1,0:T(8,128)} %reshape.286, s32[72]{0:T(128)S(1)} %add_select_fusion.1, pred[72]{0:T(512)(128)(4,1)S(1)} %iota_compare_fusion), kind=kOutput, calls=%fused_computation.17 | convolution fusion | flops 645024384 | bytes 5972328 | tf_op jit(solution)/shard_map/pmk,kr->prm/dot_general | solution.py:54
  207.3 5.8 %reshape.287 = f32[2,5184,72]{2,1,0:T(8,128)} reshape(f32[2,72,5184]{2,1,0:T(8,128)} %convolution_bitcast_fusion.11) | data formatting | bytes 5971968 | tf_op jit(solution)/shard_map/reshape | solution.py:66
  213.1 9.7 %convolution_bitcast_fusion.10 = f32[2,72,5184]{2,1,0:T(8,128)} fusion(f32[2,5184,72]{2,1,0:T(8,128)} %reshape.287, s32[72]{0:T(128)S(1)} %add_select_fusion.1, pred[72]{0:T(512)(128)(4,1)S(1)} %iota_compare_fusion), kind=kOutput, calls=%fused_computation.16 | convolution fusion | flops 645024384 | bytes 5972328 | tf_op jit(solution)/shard_map/pmk,kr->prm/dot_general | solution.py:54
  222.8 6.2 %reshape_reshape.10 = f32[2,5184,72]{2,1,0:T(8,128)} reshape(f32[2,72,5184]{2,1,0:T(8,128)} %get-tuple-element.10) | data formatting | bytes 5971968 | tf_op jit(solution)/shard_map/reshape;reshape | solution.py:60
  229.0 9.3 %convolution_bitcast_fusion.9 = f32[2,72,5184]{2,1,0:T(8,128)} fusion(f32[2,5184,72]{2,1,0:T(8,128)} %reshape_reshape.10, s32[72]{0:T(128)S(1)} %add_select_fusion.1, pred[72]{0:T(512)(128)(4,1)S(1)} %iota_compare_fusion), kind=kOutput, calls=%fused_computation.15 | convolution fusion | flops 645024384 | bytes 5972328 | tf_op jit(solution)/shard_map/pmc,kc->pkm/dot_general | solution.py:50
  238.3 5.8 %reshape.288 = f32[2,5184,72]{2,1,0:T(8,128)} reshape(f32[2,72,5184]{2,1,0:T(8,128)} %convolution_bitcast_fusion.9) | data formatting | bytes 5971968 | tf_op jit(solution)/shard_map/reshape | solution.py:61
  244.2 9.3 %convolution_bitcast_fusion.8 = f32[2,72,5184]{2,1,0:T(8,128)} fusion(f32[2,5184,72]{2,1,0:T(8,128)} %reshape.288, s32[72]{0:T(128)S(1)} %add_select_fusion.1, pred[72]{0:T(512)(128)(4,1)S(1)} %iota_compare_fusion), kind=kOutput, calls=%fused_computation.14 | convolution fusion | flops 645024384 | bytes 5972328 | tf_op jit(solution)/shard_map/pmc,kc->pkm/dot_general | solution.py:50
  253.5 6.0 %reshape.289 = f32[2,5184,72]{2,1,0:T(8,128)} reshape(f32[2,72,5184]{2,1,0:T(8,128)} %convolution_bitcast_fusion.8) | data formatting | bytes 5971968 | tf_op jit(solution)/shard_map/reshape | solution.py:62
  259.5 9.3 %fusion.1 = f32[2,72,5184]{2,1,0:T(8,128)} fusion(f32[2,5184,72]{2,1,0:T(8,128)} %reshape.289, f32[72,5184]{1,0:T(8,128)S(1)} %fusion.5, s32[72]{0:T(128)S(1)} %add_select_fusion.1, pred[72]{0:T(512)(128)(4,1)S(1)} %iota_compare_fusion), kind=kOutput, calls=%fused_computation.4 | convolution fusion | flops 645770880 | bytes 7465320 | tf_op jit(solution)/shard_map/pmc,kc->pkm/dot_general | solution.py:50
  268.8 5.8 %reshape.290 = f32[2,5184,72]{2,1,0:T(8,128)} reshape(f32[2,72,5184]{2,1,0:T(8,128)} %fusion.1) | data formatting | bytes 5971968 | tf_op jit(solution)/shard_map/reshape | solution.py:64
  274.6 9.6 %convolution_bitcast_fusion.7 = f32[2,72,5184]{2,1,0:T(8,128)} fusion(f32[2,5184,72]{2,1,0:T(8,128)} %reshape.290, s32[72]{0:T(128)S(1)} %add_select_fusion.1, pred[72]{0:T(512)(128)(4,1)S(1)} %iota_compare_fusion), kind=kOutput, calls=%fused_computation.13 | convolution fusion | flops 645024384 | bytes 5972328 | tf_op jit(solution)/shard_map/pmk,kr->prm/dot_general | solution.py:54
  284.2 6.0 %reshape.291 = f32[2,5184,72]{2,1,0:T(8,128)} reshape(f32[2,72,5184]{2,1,0:T(8,128)} %convolution_bitcast_fusion.7) | data formatting | bytes 5971968 | tf_op jit(solution)/shard_map/reshape | solution.py:65
  290.2 9.6 %convolution_bitcast_fusion.6 = f32[2,72,5184]{2,1,0:T(8,128)} fusion(f32[2,5184,72]{2,1,0:T(8,128)} %reshape.291, s32[72]{0:T(128)S(1)} %add_select_fusion.1, pred[72]{0:T(512)(128)(4,1)S(1)} %iota_compare_fusion), kind=kOutput, calls=%fused_computation.12 | convolution fusion | flops 645024384 | bytes 5972328 | tf_op jit(solution)/shard_map/pmk,kr->prm/dot_general | solution.py:54
  299.8 5.8 %reshape.292 = f32[2,5184,72]{2,1,0:T(8,128)} reshape(f32[2,72,5184]{2,1,0:T(8,128)} %convolution_bitcast_fusion.6) | data formatting | bytes 5971968 | tf_op jit(solution)/shard_map/reshape | solution.py:66
  305.6 9.6 %convolution_bitcast_fusion.5 = f32[2,72,5184]{2,1,0:T(8,128)} fusion(f32[2,5184,72]{2,1,0:T(8,128)} %reshape.292, s32[72]{0:T(128)S(1)} %add_select_fusion.1, pred[72]{0:T(512)(128)(4,1)S(1)} %iota_compare_fusion), kind=kOutput, calls=%fused_computation.11 | convolution fusion | flops 645024384 | bytes 5972328 | tf_op jit(solution)/shard_map/pmk,kr->prm/dot_general | solution.py:54
  315.2 6.2 %reshape_reshape.11 = f32[2,5184,72]{2,1,0:T(8,128)} reshape(f32[2,72,5184]{2,1,0:T(8,128)} %get-tuple-element.11) | data formatting | bytes 5971968 | tf_op jit(solution)/shard_map/reshape;reshape | solution.py:60
  321.4 9.4 %convolution_bitcast_fusion.4 = f32[2,72,5184]{2,1,0:T(8,128)} fusion(f32[2,5184,72]{2,1,0:T(8,128)} %reshape_reshape.11, s32[72]{0:T(128)S(1)} %add_select_fusion.1, pred[72]{0:T(512)(128)(4,1)S(1)} %iota_compare_fusion), kind=kOutput, calls=%fused_computation.10 | convolution fusion | flops 645024384 | bytes 5972328 | tf_op jit(solution)/shard_map/pmc,kc->pkm/dot_general | solution.py:50
  330.8 5.8 %reshape.293 = f32[2,5184,72]{2,1,0:T(8,128)} reshape(f32[2,72,5184]{2,1,0:T(8,128)} %convolution_bitcast_fusion.4) | data formatting | bytes 5971968 | tf_op jit(solution)/shard_map/reshape | solution.py:61
  336.7 9.4 %convolution_bitcast_fusion.3 = f32[2,72,5184]{2,1,0:T(8,128)} fusion(f32[2,5184,72]{2,1,0:T(8,128)} %reshape.293, s32[72]{0:T(128)S(1)} %add_select_fusion.1, pred[72]{0:T(512)(128)(4,1)S(1)} %iota_compare_fusion), kind=kOutput, calls=%fused_computation.9 | convolution fusion | flops 645024384 | bytes 5972328 | tf_op jit(solution)/shard_map/pmc,kc->pkm/dot_general | solution.py:50
  346.1 6.0 %reshape.294 = f32[2,5184,72]{2,1,0:T(8,128)} reshape(f32[2,72,5184]{2,1,0:T(8,128)} %convolution_bitcast_fusion.3) | data formatting | bytes 5971968 | tf_op jit(solution)/shard_map/reshape | solution.py:62
  352.1 9.4 %fusion.2 = f32[2,72,5184]{2,1,0:T(8,128)} fusion(f32[2,5184,72]{2,1,0:T(8,128)} %reshape.294, f32[72,5184]{1,0:T(8,128)S(1)} %fusion.5, s32[72]{0:T(128)S(1)} %add_select_fusion.1, pred[72]{0:T(512)(128)(4,1)S(1)} %iota_compare_fusion), kind=kOutput, calls=%fused_computation.5 | convolution fusion | flops 645770880 | bytes 7465320 | tf_op jit(solution)/shard_map/pmc,kc->pkm/dot_general | solution.py:50
  361.5 5.8 %reshape.295 = f32[2,5184,72]{2,1,0:T(8,128)} reshape(f32[2,72,5184]{2,1,0:T(8,128)} %fusion.2) | data formatting | bytes 5971968 | tf_op jit(solution)/shard_map/reshape | solution.py:64
  367.3 8.0 %convolution_bitcast_fusion.2 = f32[2,72,5184]{2,1,0:T(8,128)S(1)} fusion(f32[2,5184,72]{2,1,0:T(8,128)} %reshape.295, s32[72]{0:T(128)S(1)} %add_select_fusion.1, pred[72]{0:T(512)(128)(4,1)S(1)} %iota_compare_fusion), kind=kOutput, calls=%fused_computation.8 | convolution fusion | flops 645024384 | bytes 5972328 | tf_op jit(solution)/shard_map/pmk,kr->prm/dot_general | solution.py:54
  375.4 4.4 reshape.296
  379.8 9.7 %convolution_bitcast_fusion.1 = f32[2,72,5184]{2,1,0:T(8,128)} fusion(f32[2,5184,72]{2,1,0:T(8,128)} %reshape.296, s32[72]{0:T(128)S(1)} %add_select_fusion.1, pred[72]{0:T(512)(128)(4,1)S(1)} %iota_compare_fusion), kind=kOutput, calls=%fused_computation.7 | convolution fusion | flops 645024384 | bytes 5972328 | tf_op jit(solution)/shard_map/pmk,kr->prm/dot_general | solution.py:54
  389.5 6.2 %reshape.297 = f32[2,5184,72]{2,1,0:T(8,128)} reshape(f32[2,72,5184]{2,1,0:T(8,128)} %convolution_bitcast_fusion.1) | data formatting | bytes 5971968 | tf_op jit(solution)/shard_map/reshape | solution.py:66
  395.7 13.0 %multiply_reduce_fusion = (f32[72,5184]{1,0:T(8,128)S(1)}, f32[72,5184]{1,0:T(8,128)S(1)}, f32[72,5184]{1,0:T(8,128)S(1)}, f32[2,72,5184]{2,1,0:T(8,128)S(1)}) fusion(f32[2,72,5184]{2,0,1:T(2,128)S(1)} %copy-done.1, f32[2,72,5184]{2,1,0:T(8,128)} %convolution_bitcast_fusion.10, f32[2,72,5184]{2,1,0:T(8,128)} %convolution_bitcast_fusion.5, ...), kind=kOutput, calls=%fused_computation.21 | convolution fusion | flops 654355584 | bytes 23888232 | tf_op jit(solution)/shard_map/pmk,kr->prm/dot_general | solution.py:54
  408.9 20.7 %collective-permute-done.3 = f32[1,72,5184]{2,1,0:T(8,128)S(1)} collective-permute-done((f32[1,72,5184]{2,1,0:T(8,128)S(1)}, f32[1,72,5184]{2,1,0:T(8,128)S(1)}, u32[]{:S(2)}, u32[]{:S(2)}) %collective-permute-start.3) | collective-permute-done | bytes 1493024 | tf_op jit(solution)/shard_map/ppermute | solution.py:18
  430.4 20.0 %collective-permute-done.4 = f32[1,72,5184]{2,1,0:T(8,128)S(1)} collective-permute-done((f32[1,72,5184]{2,1,0:T(8,128)S(1)}, f32[1,72,5184]{2,1,0:T(8,128)S(1)}, u32[]{:S(2)}, u32[]{:S(2)}) %collective-permute-start.4) | collective-permute-done | bytes 1493024 | tf_op jit(solution)/shard_map/ppermute | solution.py:18
  450.6 18.3 %collective-permute-start.5 = (f32[1,72,5184]{2,1,0:T(8,128)S(1)}, f32[1,72,5184]{2,1,0:T(8,128)S(1)}, u32[]{:S(2)}, u32[]{:S(2)}) collective-permute-start(f32[1,72,5184]{2,1,0:T(8,128)S(1)} %bitcast_add_fusion), channel_id=1, source_target_pairs={{0,122},{2,124},{4,126},{6,0},{8,2},{10,4},{12,6},{14,8},{16,10},{... | collective-permute-start | bytes 4478984 | tf_op jit(solution)/shard_map/ppermute | solution.py:18
  468.9 22.2 %collective-permute-done.5 = f32[1,72,5184]{2,1,0:T(8,128)S(1)} collective-permute-done((f32[1,72,5184]{2,1,0:T(8,128)S(1)}, f32[1,72,5184]{2,1,0:T(8,128)S(1)}, u32[]{:S(2)}, u32[]{:S(2)}) %collective-permute-start.5) | collective-permute-done | bytes 1493024 | tf_op jit(solution)/shard_map/ppermute | solution.py:18
  493.0 36.4 %all_to_all.5 = f32[2,2,36,5184]{3,1,2,0:T(2,128)S(1)} all-to-all(f32[2,2,36,5184]{3,1,2,0:T(2,128)S(1)} %bitcast.126), channel_id=1, replica_groups=mesh['band'=64,'grid'=2] {'grid'}, dimensions={0} | all-to-all | bytes 5971968 | tf_op jit(solution)/shard_map/all_to_all | solution.py:28
  529.4 4.0 reduce_sum.41
  (44 shorter events, 17.0 us)
Async XLA Ops:
  6.5 50.6 %all-gather.2.cloned.1.call-start = ((), (), s32[]{:S(2)}) async-start(), calls=%async_computation.1 | async-start | bytes 4534272 | tf_op jit(solution)/shard_map/all_gather | solution.py:85
  60.2 20.8 %collective-permute-start = (f32[1,72,5184]{2,0,1:T(1,128)S(1)}, f32[1,72,5184]{2,0,1:T(1,128)S(1)}, u32[]{:S(2)}, u32[]{:S(2)}) collective-permute-start(f32[1,72,5184]{2,0,1:T(1,128)S(1)} %constant_dynamic-slice_fusion), channel_id=1, source_target_pairs={{0,2},{2,4},{4,6},{6,8},{8,10},{10,12},{12,14},{14,16},{16,18},{18... | collective-permute-start | bytes 4478984 | tf_op jit(solution)/shard_map/ppermute | solution.py:18
  81.0 1.1 copy-start.5
  82.1 20.8 %collective-permute-start.1 = (f32[1,72,5184]{2,0,1:T(1,128)S(1)}, f32[1,72,5184]{2,0,1:T(1,128)}, u32[]{:S(2)}, u32[]{:S(2)}) collective-permute-start(f32[1,72,5184]{2,0,1:T(1,128)S(1)} %collective-permute-done), channel_id=1, source_target_pairs={{0,2},{2,4},{4,6},{6,8},{8,10},{10,12},{12,14},{14,16},{16,18},{18... | collective-permute-start | bytes 4478984 | tf_op jit(solution)/shard_map/ppermute | solution.py:18
  102.9 21.0 %collective-permute-start.2 = (f32[1,72,5184]{2,0,1:T(1,128)}, f32[1,72,5184]{2,0,1:T(1,128)}, u32[]{:S(2)}, u32[]{:S(2)}) collective-permute-start(f32[1,72,5184]{2,0,1:T(1,128)} %collective-permute-done.1), channel_id=1, source_target_pairs={{0,2},{2,4},{4,6},{6,8},{8,10},{10,12},{12,14},{14,16},{16,18},{18... | collective-permute-start | bytes 4478984 | tf_op jit(solution)/shard_map/ppermute | solution.py:18
  108.6 2.5 copy-start.6
  111.2 14.3 %copy-start.2 = (f32[1,72,5184]{2,1,0:T(8,128)}, f32[1,72,5184]{2,1,0:T(8,128)S(1)}, u32[]{:S(2)}) copy-start(f32[1,72,5184]{2,1,0:T(8,128)S(1)} %copy.143) | copy-start | bytes 4478980
  111.2 14.3 %copy-start = (f32[2,72,5184]{2,0,1:T(2,128)S(1)}, f32[2,72,5184]{2,0,1:T(2,128)}, u32[]{:S(2)}) copy-start(f32[2,72,5184]{2,0,1:T(2,128)} %all-gather.2.cloned.1.call-done) | copy-start | bytes 8957956
  113.3 16.3 %copy-start.3 = (f32[1,72,5184]{2,1,0:T(8,128)}, f32[1,72,5184]{2,1,0:T(8,128)S(1)}, u32[]{:S(2)}) copy-start(f32[1,72,5184]{2,1,0:T(8,128)S(1)} %copy.142) | copy-start | bytes 4478980
  125.4 4.1 copy-start.4
  389.5 6.2 %copy-start.1 = (f32[2,72,5184]{2,0,1:T(2,128)S(1)}, f32[2,72,5184]{2,0,1:T(2,128)}, u32[]{:S(2)}) copy-start(f32[2,72,5184]{2,0,1:T(2,128)} %all-gather.2.cloned.1.call-done) | copy-start | bytes 8957956
  408.8 20.8 %collective-permute-start.3 = (f32[1,72,5184]{2,1,0:T(8,128)S(1)}, f32[1,72,5184]{2,1,0:T(8,128)S(1)}, u32[]{:S(2)}, u32[]{:S(2)}) collective-permute-start(f32[1,72,5184]{2,1,0:T(8,128)S(1)} %negate_bitcast_fusion), channel_id=1, source_target_pairs={{0,2},{2,4},{4,6},{6,8},{8,10},{10,12},{12,14},{14,16},{16,18},{18... | collective-permute-start | bytes 4478984 | tf_op jit(solution)/shard_map/ppermute | solution.py:18
  429.7 20.8 %collective-permute-start.4 = (f32[1,72,5184]{2,1,0:T(8,128)S(1)}, f32[1,72,5184]{2,1,0:T(8,128)S(1)}, u32[]{:S(2)}, u32[]{:S(2)}) collective-permute-start(f32[1,72,5184]{2,1,0:T(8,128)S(1)} %bitcast_add_fusion.1), channel_id=1, source_target_pairs={{0,2},{2,4},{4,6},{6,8},{8,10},{10,12},{12,14},{14,16},{16,18},{18... | collective-permute-start | bytes 4478984 | tf_op jit(solution)/shard_map/ppermute | solution.py:18
  450.6 40.5 %collective-permute-start.5 = (f32[1,72,5184]{2,1,0:T(8,128)S(1)}, f32[1,72,5184]{2,1,0:T(8,128)S(1)}, u32[]{:S(2)}, u32[]{:S(2)}) collective-permute-start(f32[1,72,5184]{2,1,0:T(8,128)S(1)} %bitcast_add_fusion), channel_id=1, source_target_pairs={{0,122},{2,124},{4,126},{6,0},{8,2},{10,4},{12,6},{14,8},{16,10},{... | collective-permute-start | bytes 4478984 | tf_op jit(solution)/shard_map/ppermute | solution.py:18
Sparse Core Ops, SparseCore 0:
  9.0 48.0 all-gather.1
where the time goes:
time: 548 us; the launch traced here: 541 us
  matrix products  173 us (32%)
  waiting for transfers between devices  165 us (30%)
  local copies, waits for them, and re-layouts  121 us (22%)
  blocking collectives  36.4 us (7%)
  starting transfers between devices  19.2 us (4%)
  between operations  14.1 us (3%)
  other arithmetic  11.4 us (2%)
    ppermute x6, waiting for transfers between devices, shifted(): return lax.ppermute(value, axis, pairs)  115 us
    dot_general x9, matrix products, inverse_axis(): jnp.einsum('pmk,kr->prm', values, table, precision=lax.Precision.HIGHEST)  88.6 us
    dot_general x9, matrix products, forward_axis(): jnp.einsum('pmc,kc->pkm', values, table, precision=lax.Precision.HIGHEST)  84.5 us
    reshape x9, local copies, waits for them, and re-layouts, coulomb_filter(): work = inverse_axis(work.reshape(pairs, count * count, count), table)  51.8 us
    all_gather x1, waiting for transfers between devices, local(): whole = lax.all_gather(bands, 'grid', axis=1, tiled=True)  49.8 us
    all_to_all x1, blocking collectives, sent_and_summed(): lax.all_to_all(split_up(array, dim, devices), axis, 0, 0, tiled=True)  36.4 us
    reshape x6, local copies, waits for them, and re-layouts, coulomb_filter(): work = forward_axis(work.reshape(pairs, count * count, count), table)  35.4 us
    ppermute x6, starting transfers between devices, shifted(): return lax.ppermute(value, axis, pairs)  19.2 us
  transfers between devices with their start and end apart: 7, of which 7 were waited for; matrix products, arithmetic and copies ran while one was open for 2% of the time, Pallas kernels for 0%

commit v1 on v0

v1 whole, which is shorter than its diff:
```python
import functools
import math

import jax
import jax.numpy as jnp
import numpy as np
from jax import lax
from jax.experimental import pallas as pl
from jax.experimental.pallas import tpu as pltpu
from jax.sharding import PartitionSpec as P

N = 72
HALF = 36
LANES = 128
ROWS = N * N
PLANE = N * N
STEPS = 3
STRIP = 8
spacing = 0.5167


def shifted(value, axis, steps):
    count = lax.axis_size(axis)
    pairs = [(source, (source + steps) % count) for source in range(count)]
    return lax.ppermute(value, axis, pairs)


def split_up(array, dim, devices):
    before, after = (array.shape[:dim], array.shape[dim + 1 :])
    return jnp.moveaxis(array.reshape(*before, devices, -1, *after), dim, 0)


def sent_and_summed(array, axis, dim):
    devices = lax.axis_size(axis)
    blocks = lax.all_to_all(split_up(array, dim, devices), axis, 0, 0, tiled=True)
    return jnp.sum(blocks, axis=0)


def rounded(x):
    return x.astype(jnp.bfloat16).astype(np.float32)


def constants():
    index = np.arange(N)
    freq = np.where(index <= HALF, index, index - HALF)
    phase = (freq[:, None] * index[None, :] % N) * (2.0 * math.pi / N)
    table = np.where(index[:, None] <= HALF, np.cos(phase), np.sin(phase)).astype(np.float32)

    def stacked(t):
        return np.concatenate([t, t, t - rounded(t)], axis=1)

    def blocks(m):
        wide = np.zeros((2 * N, 2 * LANES), np.float32)
        wide[:N, :N] = m
        wide[N:, LANES : LANES + N] = m
        return np.stack([rounded(wide), rounded(wide - rounded(wide))])

    return stacked(table), stacked(table.T), blocks(table.T), blocks(table.T).transpose(0, 2, 1)


def dot(a, b):
    return jnp.dot(a, b, preferred_element_type=jnp.float32, precision=lax.Precision.DEFAULT)


def low_part(x):
    return x - x.astype(jnp.bfloat16).astype(jnp.float32)


def down(table, x):
    return dot(table, jnp.concatenate([x, low_part(x), x], axis=0))


def along(x, high, low):
    return dot(x, high) + dot(low_part(x), high) + dot(x, low)


def fill_tables(wide_ahead, wide_back, lane_ahead, lane_back, factors):
    rows = lax.broadcasted_iota(jnp.int32, (2 * N, 2 * LANES), 0)
    cols = lax.broadcasted_iota(jnp.int32, (2 * N, 2 * LANES), 1)
    for u in range(8):
        start = 2 * N * u % LANES
        move = jnp.where(cols == rows + start, 1.0, 0.0)
        for part in range(2):
            lane_ahead[u, part] = jnp.zeros((2 * LANES, 2 * LANES), jnp.float32)
            lane_ahead[u, part, start : start + 2 * N, :] = wide_ahead[part]
            lane_back[u, part] = dot(wide_back[part], move)

    def wave(i):
        f = jnp.where(i <= HALF, i, i - HALF)
        return (f * f).astype(jnp.float32), jnp.where((i == 0) | (i == HALF), 1.0, 2.0).astype(jnp.float32)

    factor = (2.0 * math.pi / (N * spacing)) ** 2
    square_b, weight_b = wave(lax.broadcasted_iota(jnp.int32, (N, LANES), 0))
    square_c, weight_c = wave(lax.broadcasted_iota(jnp.int32, (N, LANES), 1))
    inside = lax.broadcasted_iota(jnp.int32, (N, LANES), 1) < N

    def fill(i, _):
        square_a, weight_a = wave(i)
        ksq = factor * (square_a + square_b + square_c)
        keep = (ksq > 0) & inside
        coulomb = jnp.where(keep, 4.0 * math.pi / jnp.where(keep, ksq, 1.0), 0.0)
        factors[pl.ds(pl.multiple_of(i * N, 8), N), :] = coulomb * (weight_a * weight_b * weight_c) / float(N**3)
        return 0

    lax.fori_loop(0, N, fill, 0)


def exchange(homes, visit, home_outs, visit_out, first, ahead, back, lane_ahead, lane_back, factors, u, w):
    BODY = 5
    WIDE = 2 * LANES
    TAIL = PLANE // WIDE * WIDE

    def flat_ahead(tiles):
        for at, width in tiles:
            for p in range(2):
                x = homes[p][:, pl.ds(at, width)] * visit[:, pl.ds(at, width)]
                if width < LANES:
                    x = jnp.concatenate([x, jnp.zeros((N, LANES - width), jnp.float32)], axis=1)
                u[p, :, pl.ds(at, max(width, LANES))] = down(ahead[...], x)

    def wide_tiles(i):
        return [(pl.multiple_of((i * BODY + k) * WIDE, LANES), WIDE) for k in range(BODY)]

    def pass_1(i, _):
        flat_ahead(wide_tiles(i))
        return 0

    lax.fori_loop(0, TAIL // WIDE // BODY, pass_1, 0)
    flat_ahead([(TAIL, PLANE - TAIL)])

    def lines_ahead(t, count):
        base = pl.multiple_of(t * 9 * LANES, LANES)
        for k in range(count):
            at = 2 * N * k // LANES * LANES
            x = jnp.concatenate([u[p, :, pl.ds(base + at, WIDE)] for p in range(2)], axis=0)
            y = along(x, lane_ahead[k, 0], lane_ahead[k, 1])
            r = pl.multiple_of((t * 8 + k) * 2 * N, 8)
            for p in range(2):
                w[p, pl.ds(r, N), :] = y[N * p : N * (p + 1), :LANES]
                w[p, pl.ds(r + N, N), :] = y[N * p : N * (p + 1), LANES:]

    def pass_2(t, _):
        lines_ahead(t, 8)
        return 0

    lax.fori_loop(0, 4, pass_2, 0)
    lines_ahead(4, 4)

    def load_w(i):
        rows = pl.ds(i, N, stride=N)
        return jnp.concatenate([w[0, rows, :], w[1, rows, :]], axis=1)

    def store_w(i, y):
        rows = pl.ds(i, N, stride=N)
        w[0, rows, :] = y[:, :LANES]
        w[1, rows, :] = y[:, LANES:]

    def ahead_b(i, x):
        y = down(ahead[...], x)
        f = factors[pl.ds(pl.multiple_of(i * N, 8), N), :]
        return y * jnp.concatenate([f, f], axis=1)

    def pass_3(i, _):
        now = [i * STRIP + k for k in range(STRIP)]
        before = [i * STRIP - STRIP + k for k in range(STRIP)]
        xs, ys = [load_w(q) for q in now], [load_w(q) for q in before]
        xs = [ahead_b(q, x) for q, x in zip(now, xs)]
        ys = [down(back[...], y) for y in ys]
        for q, x in zip(now, xs):
            store_w(q, x)
        for q, y in zip(before, ys):
            store_w(q, y)
        return 0

    for q, x in [(q, ahead_b(q, load_w(q))) for q in range(STRIP)]:
        store_w(q, x)
    lax.fori_loop(1, N // STRIP, pass_3, 0)
    for q, y in [(q, down(back[...], load_w(q))) for q in range(N - STRIP, N)]:
        store_w(q, y)

    def lines_back(t, count):
        base = pl.multiple_of(t * 9 * LANES, LANES)
        total = {}
        for k in range(count):
            tile = 2 * N * k // LANES
            r = pl.multiple_of((t * 8 + k) * 2 * N, 8)
            x = jnp.concatenate(
                [jnp.concatenate([w[p, pl.ds(r, N), :], w[p, pl.ds(r + N, N), :]], axis=1) for p in range(2)], axis=0
            )
            y = along(x, lane_back[k, 0], lane_back[k, 1])
            for half in range(2):
                part = y[:, LANES * half : LANES * (half + 1)]
                total[tile + half] = total[tile + half] + part if tile + half in total else part
        for tile, value in total.items():
            for p in range(2):
                u[p, :, pl.ds(base + tile * LANES, LANES)] = value[N * p : N * (p + 1)]

    def pass_4(t, _):
        lines_back(t, 8)
        return 0

    lax.fori_loop(0, 4, pass_4, 0)
    lines_back(4, 4)

    def flat_back(tiles):
        for at, width in tiles:
            cells = pl.ds(at, width)
            total = None
            for p in range(2):
                v = down(back[...], u[p, :, pl.ds(at, max(width, LANES))])[:, :width]
                mine = v * visit[:, cells]
                home_outs[p][:, cells] = -mine if first else home_outs[p][:, cells] - mine
                part = v * homes[p][:, cells]
                total = part if total is None else total + part
            visit_out[:, cells] = -total

    def pass_5(i, _):
        flat_back(wide_tiles(i))
        return 0

    lax.fori_loop(0, TAIL // WIDE // BODY, pass_5, 0)
    flat_back([(TAIL, PLANE - TAIL)])


def kernel(
    home_in, visit_in, ahead, back, wide_ahead, wide_back, home_out, visit_out,
    flat, outs, lane_ahead, lane_back, factors, u, w, sems,
):
    copies = [pltpu.make_async_copy(home_in.at[i], flat.at[i], sems.at[i]) for i in range(2)]
    copies += [pltpu.make_async_copy(visit_in.at[i], flat.at[2 + i], sems.at[2 + i]) for i in range(3)]
    for copy in copies:
        copy.start()
    fill_tables(wide_ahead, wide_back, lane_ahead, lane_back, factors)
    for copy in copies:
        copy.wait()
    for j in range(3):
        exchange(
            [flat.at[0], flat.at[1]], flat.at[2 + j], [outs.at[0], outs.at[1]], outs.at[2 + j], j == 0,
            ahead, back, lane_ahead, lane_back, factors, u, w,
        )
    copies = [pltpu.make_async_copy(outs.at[i], home_out.at[i], sems.at[i]) for i in range(2)]
    copies += [pltpu.make_async_copy(outs.at[2 + i], visit_out.at[i], sems.at[2 + i]) for i in range(3)]
    for copy in copies:
        copy.start()
    for copy in copies:
        copy.wait()


def pair_terms(home, visit, consts):
    hbm = pl.BlockSpec(memory_space=pl.ANY)
    vmem = pl.BlockSpec(memory_space=pltpu.VMEM)
    return pl.pallas_call(
        kernel,
        out_shape=(
            jax.ShapeDtypeStruct((2, N, PLANE), jnp.float32),
            jax.ShapeDtypeStruct((3, N, PLANE), jnp.float32),
        ),
        in_specs=[hbm, hbm, vmem, vmem, vmem, vmem],
        out_specs=(hbm, hbm),
        scratch_shapes=[
            pltpu.VMEM((5, N, PLANE), jnp.float32),
            pltpu.VMEM((5, N, PLANE), jnp.float32),
            pltpu.VMEM((8, 2, 2 * LANES, 2 * LANES), jnp.float32),
            pltpu.VMEM((8, 2, 2 * LANES, 2 * LANES), jnp.float32),
            pltpu.VMEM((ROWS, LANES), jnp.float32),
            pltpu.VMEM((2, N, 41 * LANES), jnp.float32),
            pltpu.VMEM((2, ROWS, LANES), jnp.float32),
            pltpu.SemaphoreType.DMA((5,)),
        ],
        compiler_params=pltpu.CompilerParams(vmem_limit_bytes=60 * 1024 * 1024),
        name="pair_terms",
    )(home, visit, *consts)


def local(bands):
    consts = constants()
    whole = lax.all_gather(bands, "grid", axis=1, tiled=True)
    share = whole.shape[0] // lax.axis_size("grid")
    first = lax.axis_index("grid") * share
    visit = lax.dynamic_slice_in_dim(whole, first, share, 0)
    visits = jnp.concatenate([shifted(visit, "band", s) for s in (1, 2, 3)], axis=0)
    home_total, parts = pair_terms(whole, visits, consts)
    carried = sum(shifted(parts[s : s + 1], "band", -(s + 1)) for s in range(3))
    own_rows = lax.dynamic_slice_in_dim(home_total, first, share, 0) + carried
    home_total = lax.dynamic_update_slice_in_dim(home_total, own_rows, first, 0)
    return sent_and_summed(home_total, "grid", 1)


def solution(mesh):
    return jax.shard_map(
        local,
        mesh=mesh,
        in_specs=(P("band", "grid", None),),
        out_specs=P("band", "grid", None),
        check_vma=False,
    )
```

time: 548 us -> 331 us (0.60); the launches traced: 541 us -> 330 us
  matrix products: 173 us -> 0 us
  local copies, waits for them, and re-layouts: 121 us -> 7.92 us
  Pallas kernels: 0 us -> 48.4 us
  waiting for transfers between devices: 165 us -> 188 us
  starting transfers between devices: 19.2 us -> 27.4 us
    dot_general x18 -> x0, matrix products: 173 us -> none  [the longest x9 88.6 us: inverse_axis(): jnp.einsum('pmk,kr->prm', values, table, precision=lax.Precision.HIGHEST)]
    reshape x15 -> x0, local copies, waits for them, and re-layouts: 87.2 us -> none  [the longest x9 51.8 us: coulomb_filter(): work = inverse_axis(work.reshape(pairs, count * count, count), table)]
    pallas_call x0 -> x1, Pallas kernels: none -> 48.4 us  [pair_terms(): pl.pallas_call(kernel, out_shape=(jax.ShapeDtypeStruct((2, N, PLANE), jnp...]
    ppermute x6, waiting for transfers between devices: 115 us -> 137 us  [shifted(): return lax.ppermute(value, axis, pairs)]
    another operation x3 -> x0, local copies, waits for them, and re-layouts: 18.8 us -> none  [coulomb_filter(): work = forward_axis(density.reshape(pairs, count * count, count), table)]
    ppermute x6, starting transfers between devices: 19.2 us -> 27.4 us  [shifted(): return lax.ppermute(value, axis, pairs)]
  transfers between devices with their start and end apart: 7 -> 7, of which waited for: 7 -> 6; matrix products, arithmetic and copies ran while one was open for 2% -> 0% of each run, Pallas kernels for 0% -> 0%
where the time goes in v1:
time: 331 us; the launch traced here: 330 us
  waiting for transfers between devices  188 us (57%)
  Pallas kernels  48.4 us (15%)
  blocking collectives  37.9 us (11%)
  starting transfers between devices  27.4 us (8%)
  between operations  13.5 us (4%)
  local copies, waits for them, and re-layouts  7.92 us (2%)
  other arithmetic  6.81 us (2%)
    ppermute x6, waiting for transfers between devices, shifted(): return lax.ppermute(value, axis, pairs)  137 us
    all_gather x1, waiting for transfers between devices, local(): whole = lax.all_gather(bands, 'grid', axis=1, tiled=True)  49.8 us
    pallas_call x1, Pallas kernels, pair_terms(): pl.pallas_call(kernel, out_shape=(jax.ShapeDtypeStruct((2, N, PLANE), jnp...  48.4 us
    all_to_all x1, blocking collectives, sent_and_summed(): lax.all_to_all(split_up(array, dim, devices), axis, 0, 0, tiled=True)  37.9 us
    ppermute x6, starting transfers between devices, shifted(): return lax.ppermute(value, axis, pairs)  27.4 us
  transfers between devices with their start and end apart: 7, of which 6 were waited for; matrix products, arithmetic and copies ran while one was open for 0% of the time, Pallas kernels for 0%

profile of v1, /device:TPU:4, one launch (start us, length us, event | category | flops | bytes accessed | tf_op | source)
XLA Modules:
  0.0 329.9 jit_solution(8637468762535345609)
XLA Ops:
  6.5 0.0 all-gather.2.cloned.1.call-start
  6.5 0.7 all-gather.2.cloned.1.call-update
  7.3 49.8 %all-gather.2.cloned.1.call-done = f32[2,72,5184]{2,0,1:T(2,128)} async-done(((f32[2,36,5184]{2,0,1:T(2,128)}), f32[2,72,5184]{2,0,1:T(2,128)}) %all-gather.2.cloned.1.call-update) | async-done | bytes 2986000 | tf_op jit(solution)/shard_map/all_gather | solution.py:277
  57.1 2.0 copy.10.home_in
  59.1 0.0 copy-start
  59.2 0.1 constant_dynamic-slice_fusion
  59.3 1.5 copy-done
  60.7 1.1 collective-permute-start.2
  61.8 2.7 collective-permute-start.1
  64.5 0.0 collective-permute-start
  64.5 29.4 %collective-permute-done.2 = f32[1,72,5184]{2,1,0:T(8,128)S(1)} collective-permute-done((f32[1,72,5184]{2,1,0:T(8,128)S(1)}, f32[1,72,5184]{2,1,0:T(8,128)S(1)}, u32[]{:S(2)}, u32[]{:S(2)}) %collective-permute-start.2) | collective-permute-done | bytes 1493024 | tf_op jit(solution)/shard_map/ppermute | solution.py:25
  93.9 34.5 %collective-permute-done.1 = f32[1,72,5184]{2,1,0:T(8,128)S(1)} collective-permute-done((f32[1,72,5184]{2,1,0:T(8,128)S(1)}, f32[1,72,5184]{2,1,0:T(8,128)S(1)}, u32[]{:S(2)}, u32[]{:S(2)}) %collective-permute-start.1) | collective-permute-done | bytes 1493024 | tf_op jit(solution)/shard_map/ppermute | solution.py:25
  128.4 1.4 collective-permute-done
  129.9 2.4 pad_maximum_fusion.visit_in
  132.2 48.4 %pair_terms.1 = (f32[2,72,5184]{2,1,0:T(8,128)}, f32[3,72,5184]{2,1,0:T(8,128)}) custom-call(f32[2,72,5184]{2,1,0:T(8,128)} %copy-done, f32[3,72,5184]{2,1,0:T(8,128)} %pad_maximum_fusion.visit_in, f32[72,216]{1,0:T(8,128)} %constant.18.clone.ahead, f32[72,216]{1,0:T(8,128)} %constant.19.clone.back, f32[2,144,256]{2,1,0:T(8,128)} %constant.20.clone.wide_ahead, ...), custom_call_target="tpu_custom_call" | custom-call | tf_op jit(solution)/shard_map/pair_terms/pallas_call | solution.py:252
  180.7 0.0 copy-start.1
  180.7 2.7 fusion
  183.4 19.1 %collective-permute-start.4 = (f32[1,72,5184]{2,1,0:T(8,128)S(1)}, f32[1,72,5184]{2,1,0:T(8,128)S(1)}, u32[]{:S(2)}, u32[]{:S(2)}) collective-permute-start(f32[1,72,5184]{2,1,0:T(8,128)S(1)} %get-tuple-element.9), channel_id=1, source_target_pairs={{0,124},{2,126},{4,0},{6,2},{8,4},{10,6},{12,8},{14,10},{16,12},{1... | collective-permute-start | bytes 4478984 | tf_op jit(solution)/shard_map/ppermute | solution.py:25
  202.5 0.0 collective-permute-start.5
  202.5 4.5 %collective-permute-start.3 = (f32[1,72,5184]{2,1,0:T(8,128)S(1)}, f32[1,72,5184]{2,1,0:T(8,128)S(1)}, u32[]{:S(2)}, u32[]{:S(2)}) collective-permute-start(f32[1,72,5184]{2,1,0:T(8,128)S(1)} %get-tuple-element.11), channel_id=1, source_target_pairs={{0,126},{2,0},{4,2},{6,4},{8,6},{10,8},{12,10},{14,12},{16,14},{18... | collective-permute-start | bytes 4478984 | tf_op jit(solution)/shard_map/ppermute | solution.py:25
  207.0 29.0 %collective-permute-done.4 = f32[1,72,5184]{2,1,0:T(8,128)S(1)} collective-permute-done((f32[1,72,5184]{2,1,0:T(8,128)S(1)}, f32[1,72,5184]{2,1,0:T(8,128)S(1)}, u32[]{:S(2)}, u32[]{:S(2)}) %collective-permute-start.4) | collective-permute-done | bytes 1493024 | tf_op jit(solution)/shard_map/ppermute | solution.py:25
  236.0 43.2 %collective-permute-done.5 = f32[1,72,5184]{2,1,0:T(8,128)S(1)} collective-permute-done((f32[1,72,5184]{2,1,0:T(8,128)S(1)}, f32[1,72,5184]{2,1,0:T(8,128)S(1)}, u32[]{:S(2)}, u32[]{:S(2)}) %collective-permute-start.5) | collective-permute-done | bytes 1493024 | tf_op jit(solution)/shard_map/ppermute | solution.py:25
  279.2 0.0 collective-permute-done.3
  279.2 0.0 copy-done.1
  279.2 0.4 add_dynamic-update-slice_fusion
  279.6 1.6 copy.11
  281.2 37.9 %all_to_all.5 = f32[2,2,36,5184]{3,1,2,0:T(2,128)S(1)} all-to-all(f32[2,2,36,5184]{3,1,2,0:T(2,128)S(1)} %bitcast.3), channel_id=1, replica_groups=mesh['band'=64,'grid'=2] {'grid'}, dimensions={0} | all-to-all | bytes 5971968 | tf_op jit(solution)/shard_map/all_to_all | solution.py:35
  319.1 4.0 %reduce_sum.9 = f32[2,36,5184]{2,0,1:T(2,128)} reduce(f32[2,2,36,5184]{3,1,2,0:T(2,128)S(1)} %all_to_all.5, f32[]{:T(128)} %constant.7.clone.1), dimensions={0}, to_apply=%region_0.0 | reduce | flops 373248 | bytes 4478980 | tf_op jit(solution)/shard_map/reduce_sum | solution.py:36
Async XLA Ops:
  6.5 50.6 %all-gather.2.cloned.1.call-start = ((), (), s32[]{:S(2)}) async-start(), calls=%async_computation.1 | async-start | bytes 4534272 | tf_op jit(solution)/shard_map/all_gather | solution.py:277
  59.1 1.6 copy-start
  60.7 33.2 %collective-permute-start.2 = (f32[1,72,5184]{2,1,0:T(8,128)S(1)}, f32[1,72,5184]{2,1,0:T(8,128)S(1)}, u32[]{:S(2)}, u32[]{:S(2)}) collective-permute-start(f32[1,72,5184]{2,1,0:T(8,128)S(1)} %constant_dynamic-slice_fusion), channel_id=1, source_target_pairs={{0,6},{2,8},{4,10},{6,12},{8,14},{10,16},{12,18},{14,20},{16,22},{... | collective-permute-start | bytes 4478984 | tf_op jit(solution)/shard_map/ppermute | solution.py:25
  61.8 66.6 %collective-permute-start.1 = (f32[1,72,5184]{2,1,0:T(8,128)S(1)}, f32[1,72,5184]{2,1,0:T(8,128)S(1)}, u32[]{:S(2)}, u32[]{:S(2)}) collective-permute-start(f32[1,72,5184]{2,1,0:T(8,128)S(1)} %constant_dynamic-slice_fusion), channel_id=1, source_target_pairs={{0,4},{2,6},{4,8},{6,10},{8,12},{10,14},{12,16},{14,18},{16,20},{1... | collective-permute-start | bytes 4478984 | tf_op jit(solution)/shard_map/ppermute | solution.py:25
  64.5 65.3 %collective-permute-start = (f32[1,72,5184]{2,1,0:T(8,128)S(1)}, f32[1,72,5184]{2,1,0:T(8,128)S(1)}, u32[]{:S(2)}, u32[]{:S(2)}) collective-permute-start(f32[1,72,5184]{2,1,0:T(8,128)S(1)} %constant_dynamic-slice_fusion), channel_id=1, source_target_pairs={{0,2},{2,4},{4,6},{6,8},{8,10},{10,12},{12,14},{14,16},{16,18},{18... | collective-permute-start | bytes 4478984 | tf_op jit(solution)/shard_map/ppermute | solution.py:25
  180.7 98.5 %copy-start.1 = (f32[2,72,5184]{2,1,0:T(8,128)S(1)}, f32[2,72,5184]{2,1,0:T(8,128)}, u32[]{:S(2)}) copy-start(f32[2,72,5184]{2,1,0:T(8,128)} %get-tuple-element.7) | copy-start | bytes 8957956
  183.4 52.6 %collective-permute-start.4 = (f32[1,72,5184]{2,1,0:T(8,128)S(1)}, f32[1,72,5184]{2,1,0:T(8,128)S(1)}, u32[]{:S(2)}, u32[]{:S(2)}) collective-permute-start(f32[1,72,5184]{2,1,0:T(8,128)S(1)} %get-tuple-element.9), channel_id=1, source_target_pairs={{0,124},{2,126},{4,0},{6,2},{8,4},{10,6},{12,8},{14,10},{16,12},{1... | collective-permute-start | bytes 4478984 | tf_op jit(solution)/shard_map/ppermute | solution.py:25
  202.5 76.7 %collective-permute-start.5 = (f32[1,72,5184]{2,1,0:T(8,128)S(1)}, f32[1,72,5184]{2,1,0:T(8,128)S(1)}, u32[]{:S(2)}, u32[]{:S(2)}) collective-permute-start(f32[1,72,5184]{2,1,0:T(8,128)S(1)} %get-tuple-element.10), channel_id=1, source_target_pairs={{0,122},{2,124},{4,126},{6,0},{8,2},{10,4},{12,6},{14,8},{16,10},{... | collective-permute-start | bytes 4478984 | tf_op jit(solution)/shard_map/ppermute | solution.py:25
  202.5 76.7 %collective-permute-start.3 = (f32[1,72,5184]{2,1,0:T(8,128)S(1)}, f32[1,72,5184]{2,1,0:T(8,128)S(1)}, u32[]{:S(2)}, u32[]{:S(2)}) collective-permute-start(f32[1,72,5184]{2,1,0:T(8,128)S(1)} %get-tuple-element.11), channel_id=1, source_target_pairs={{0,126},{2,0},{4,2},{6,4},{8,6},{10,8},{12,10},{14,12},{16,14},{18... | collective-permute-start | bytes 4478984 | tf_op jit(solution)/shard_map/ppermute | solution.py:25
Sparse Core Ops, SparseCore 0:
  9.0 48.0 all-gather.1

commit v2 on v1

--- a/solution.py
+++ b/solution.py
@@ -14,26 +14,11 @@
 LANES = 128
 ROWS = N * N
 PLANE = N * N
-STEPS = 3
+MESH = pl.DeviceIdType.MESH
+PADDED = 80
+CHUNKS = ((0, 1792), (1792, 1792), (3584, 1600))
 STRIP = 8
 spacing = 0.5167
-
-
-def shifted(value, axis, steps):
-    count = lax.axis_size(axis)
-    pairs = [(source, (source + steps) % count) for source in range(count)]
-    return lax.ppermute(value, axis, pairs)
-
-
-def split_up(array, dim, devices):
-    before, after = (array.shape[:dim], array.shape[dim + 1 :])
-    return jnp.moveaxis(array.reshape(*before, devices, -1, *after), dim, 0)
-
-
-def sent_and_summed(array, axis, dim):
-    devices = lax.axis_size(axis)
-    blocks = lax.all_to_all(split_up(array, dim, devices), axis, 0, 0, tiled=True)
-    return jnp.sum(blocks, axis=0)
 
 
 def rounded(x):
@@ -55,7 +40,10 @@
         wide[N:, LANES : LANES + N] = m
         return np.stack([rounded(wide), rounded(wide - rounded(wide))])
 
-    return stacked(table), stacked(table.T), blocks(table.T), blocks(table.T).transpose(0, 2, 1)
+    halves = np.concatenate([np.arange(HALF), np.arange(HALF) + PADDED // 2])
+    halved = np.zeros((N, PADDED), np.float32)
+    halved[:, halves] = table
+    return stacked(table), stacked(table.T), stacked(halved), stacked(halved.T), blocks(table.T), blocks(table.T).transpose(0, 2, 1)
 
 
 def dot(a, b):
@@ -68,6 +56,11 @@
 
 def down(table, x):
     return dot(table, jnp.concatenate([x, low_part(x), x], axis=0))
+
+
+def joined(x):
+    gap = jnp.zeros((PADDED // 2 - HALF, x[0].shape[1]), jnp.float32)
+    return jnp.concatenate([x[0], gap, x[1], gap], axis=0)
 
 
 def along(x, high, low):
@@ -105,7 +98,8 @@
     lax.fori_loop(0, N, fill, 0)
 
 
-def exchange(homes, visit, home_outs, visit_out, first, ahead, back, lane_ahead, lane_back, factors, u, w):
+def exchange(homes, visit, home_outs, visit_out, first, tables, lane_ahead, lane_back, factors, u, w):
+    ahead, back, half_ahead, half_back = tables
     BODY = 5
     WIDE = 2 * LANES
     TAIL = PLANE // WIDE * WIDE
@@ -113,10 +107,10 @@
     def flat_ahead(tiles):
         for at, width in tiles:
             for p in range(2):
-                x = homes[p][:, pl.ds(at, width)] * visit[:, pl.ds(at, width)]
+                x = joined([homes[p][h, :, pl.ds(at, width)] * visit[h, :, pl.ds(at, width)] for h in range(2)])
                 if width < LANES:
-                    x = jnp.concatenate([x, jnp.zeros((N, LANES - width), jnp.float32)], axis=1)
-                u[p, :, pl.ds(at, max(width, LANES))] = down(ahead[...], x)
+                    x = jnp.concatenate([x, jnp.zeros((PADDED, LANES - width), jnp.float32)], axis=1)
+                u[p, :, pl.ds(at, max(width, LANES))] = down(half_ahead[...], x)
 
     def wide_tiles(i):
         return [(pl.multiple_of((i * BODY + k) * WIDE, LANES), WIDE) for k in range(BODY)]
@@ -205,14 +199,16 @@
     def flat_back(tiles):
         for at, width in tiles:
             cells = pl.ds(at, width)
-            total = None
+            total = [0.0, 0.0]
             for p in range(2):
-                v = down(back[...], u[p, :, pl.ds(at, max(width, LANES))])[:, :width]
-                mine = v * visit[:, cells]
-                home_outs[p][:, cells] = -mine if first else home_outs[p][:, cells] - mine
-                part = v * homes[p][:, cells]
-                total = part if total is None else total + part
-            visit_out[:, cells] = -total
+                v = down(half_back[...], u[p, :, pl.ds(at, max(width, LANES))])[:, :width]
+                for h in range(2):
+                    part = v[PADDED // 2 * h : PADDED // 2 * h + HALF]
+                    mine = part * visit[h, :, cells]
+                    home_outs[p][h, :, cells] = -mine if first else home_outs[p][h, :, cells] - mine
+                    total[h] = total[h] - part * homes[p][h, :, cells]
+            for h in range(2):
+                visit_out[h, :, cells] = total[h]
 
     def pass_5(i, _):
         flat_back(wide_tiles(i))
@@ -222,68 +218,211 @@
     flat_back([(TAIL, PLANE - TAIL)])
 
 
-def kernel(
-    home_in, visit_in, ahead, back, wide_ahead, wide_back, home_out, visit_out,
+def pair_kernel(
+    own, other, visit_in, ahead, back, half_ahead, half_back, wide_ahead, wide_back, home_out, visit_out,
     flat, outs, lane_ahead, lane_back, factors, u, w, sems,
 ):
-    copies = [pltpu.make_async_copy(home_in.at[i], flat.at[i], sems.at[i]) for i in range(2)]
-    copies += [pltpu.make_async_copy(visit_in.at[i], flat.at[2 + i], sems.at[2 + i]) for i in range(3)]
+    g = lax.axis_index("grid")
+    copies = [pltpu.make_async_copy(own.at[b], flat.at[b, g], sems.at[b]) for b in range(2)]
+    copies += [pltpu.make_async_copy(other.at[b], flat.at[b, 1 - g], sems.at[2 + b]) for b in range(2)]
+    copies += [pltpu.make_async_copy(visit_in.at[i], flat.at[2 + i], sems.at[4 + i]) for i in range(3)]
     for copy in copies:
         copy.start()
     fill_tables(wide_ahead, wide_back, lane_ahead, lane_back, factors)
     for copy in copies:
         copy.wait()
+    outgoing = []
     for j in range(3):
         exchange(
             [flat.at[0], flat.at[1]], flat.at[2 + j], [outs.at[0], outs.at[1]], outs.at[2 + j], j == 0,
-            ahead, back, lane_ahead, lane_back, factors, u, w,
+            (ahead, back, half_ahead, half_back), lane_ahead, lane_back, factors, u, w,
         )
-    copies = [pltpu.make_async_copy(outs.at[i], home_out.at[i], sems.at[i]) for i in range(2)]
-    copies += [pltpu.make_async_copy(outs.at[2 + i], visit_out.at[i], sems.at[2 + i]) for i in range(3)]
-    for copy in copies:
-        copy.start()
-    for copy in copies:
+        outgoing.append(pltpu.make_async_copy(outs.at[2 + j], visit_out.at[j], sems.at[2 + j]))
+        outgoing[-1].start()
+    for b in range(2):
+        outgoing.append(pltpu.make_async_copy(outs.at[b], home_out.at[b], sems.at[b]))
+        outgoing[-1].start()
+    for copy in outgoing:
         copy.wait()
 
 
-def pair_terms(home, visit, consts):
-    hbm = pl.BlockSpec(memory_space=pl.ANY)
-    vmem = pl.BlockSpec(memory_space=pltpu.VMEM)
+HBM = pl.BlockSpec(memory_space=pl.ANY)
+VMEM = pl.BlockSpec(memory_space=pltpu.VMEM)
+
+
+def pair_terms(own, other, visit):
     return pl.pallas_call(
-        kernel,
+        pair_kernel,
         out_shape=(
-            jax.ShapeDtypeStruct((2, N, PLANE), jnp.float32),
-            jax.ShapeDtypeStruct((3, N, PLANE), jnp.float32),
+            jax.ShapeDtypeStruct((2, 2, HALF, PLANE), jnp.float32),
+            jax.ShapeDtypeStruct((3, 2, HALF, PLANE), jnp.float32),
         ),
-        in_specs=[hbm, hbm, vmem, vmem, vmem, vmem],
-        out_specs=(hbm, hbm),
+        in_specs=[HBM, HBM, HBM] + [VMEM] * 6,
+        out_specs=(HBM, HBM),
         scratch_shapes=[
-            pltpu.VMEM((5, N, PLANE), jnp.float32),
-            pltpu.VMEM((5, N, PLANE), jnp.float32),
+            pltpu.VMEM((5, 2, HALF, PLANE), jnp.float32),
+            pltpu.VMEM((5, 2, HALF, PLANE), jnp.float32),
             pltpu.VMEM((8, 2, 2 * LANES, 2 * LANES), jnp.float32),
             pltpu.VMEM((8, 2, 2 * LANES, 2 * LANES), jnp.float32),
             pltpu.VMEM((ROWS, LANES), jnp.float32),
             pltpu.VMEM((2, N, 41 * LANES), jnp.float32),
             pltpu.VMEM((2, ROWS, LANES), jnp.float32),
-            pltpu.SemaphoreType.DMA((5,)),
+            pltpu.SemaphoreType.DMA((7,)),
         ],
         compiler_params=pltpu.CompilerParams(vmem_limit_bytes=60 * 1024 * 1024),
         name="pair_terms",
-    )(home, visit, *consts)
+    )(own, other, visit, *constants())
+
+
+def places():
+    n, g, count = lax.axis_index("band"), lax.axis_index("grid"), lax.axis_size("band")
+    core = lax.rem(n, 2)
+    swap = (n, 1 - g)
+    x_to, x_from = (lax.rem(n + 2, count), 1 - g), (lax.rem(n + count - 2, count), 1 - g)
+    y_to, y_from = (lax.rem(n + 1 + 2 * core, count), g), (lax.rem(n + count - 3 + 2 * core, count), g)
+    side = (n + 1 - 2 * core, g)
+    return g, swap, x_to, x_from, y_to, y_from, side
+
+
+def meet(receivers):
+    barrier = pltpu.get_barrier_semaphore()
+    for device in receivers:
+        pl.semaphore_signal(barrier, inc=1, device_id=device, device_id_type=MESH)
+    pl.semaphore_wait(barrier, len(receivers))
+
+
+def sender(send, recv):
+    index = iter(range(64))
+
+    def make(src, dst, device):
+        i = next(index)
+        return pltpu.make_async_remote_copy(src, dst, send.at[i], recv.at[i], device_id=device, device_id_type=MESH)
+
+    return make
+
+
+def gather_kernel(bands, other, visit, send, recv):
+    g, swap, x_to, x_from, y_to, y_from, side = places()
+    meet([swap, x_from, y_from, side])
+    make = sender(send, recv)
+    f = 1 - g
+
+    def cells(c):
+        return pl.ds(*CHUNKS[c])
+
+    pieces = range(len(CHUNKS))
+    e1 = [make(bands.at[g, :, cells(c)], other.at[g, :, cells(c)], swap) for c in pieces]
+    x1 = make(bands.at[f], visit.at[0, g], x_to)
+    y1 = make(bands.at[f], visit.at[2, g], y_to)
+    e2 = make(bands.at[f], other.at[f], swap)
+    x2 = [make(other.at[f, :, cells(c)], visit.at[0, f, :, cells(c)], x_to) for c in pieces]
+    y2 = [make(other.at[f, :, cells(c)], visit.at[2, f, :, cells(c)], y_to) for c in pieces]
+    s1 = make(visit.at[0, f], visit.at[1, f], side)
+    s2 = [make(visit.at[0, g, :, cells(c)], visit.at[1, g, :, cells(c)], side) for c in pieces]
+    for copy in e1 + [x1, y1]:
+        copy.start()
+    for c in pieces:
+        e1[c].wait_recv()
+        x2[c].start()
+        y2[c].start()
+    e2.start()
+    x1.wait_recv()
+    s1.start()
+    for c in pieces:
+        x2[c].wait_recv()
+        s2[c].start()
+    y1.wait_recv()
+    for copy in y2 + [e2, s1] + s2:
+        copy.wait_recv()
+    for copy in e1 + [x1, y1, e2] + x2 + y2 + [s1] + s2:
+        copy.wait_send()
+
+
+def gathered(bands):
+    return pl.pallas_call(
+        gather_kernel,
+        out_shape=(
+            jax.ShapeDtypeStruct((2, HALF, PLANE), jnp.float32),
+            jax.ShapeDtypeStruct((3, 2, HALF, PLANE), jnp.float32),
+        ),
+        in_specs=[HBM],
+        out_specs=(HBM, HBM),
+        scratch_shapes=[pltpu.SemaphoreType.DMA((16,)), pltpu.SemaphoreType.DMA((16,))],
+        compiler_params=pltpu.CompilerParams(collective_id=0, has_side_effects=True),
+        name="gather_bands",
+    )(bands)
+
+
+def scatter_kernel(home, visit, out, near, from_s, from_x, from_y, mine, from_e, send, recv, local):
+    g, swap, x_to, x_from, y_to, y_from, side = places()
+    f = 1 - g
+    loads = [pltpu.make_async_copy(visit.at[0], near, local.at[0])]
+    loads += [pltpu.make_async_copy(home.at[b], mine.at[b], local.at[1 + b]) for b in range(2)]
+    for copy in loads:
+        copy.start()
+    meet([swap, x_to, y_to, side])
+    make = sender(send, recv)
+    pieces = range(len(CHUNKS))
+
+    def cells(c):
+        return pl.ds(*CHUNKS[c])
+
+    s = [[make(visit.at[1, h, :, cells(c)], from_s.at[h, :, cells(c)], side) for c in pieces] for h in (g, f)]
+    y = [make(visit.at[2, h], from_y.at[h], y_from) for h in (f, g)]
+    x = [[make(near.at[h, :, cells(c)], from_x.at[h, :, cells(c)], x_from) for c in pieces] for h in (g, f)]
+    e1 = make(home.at[g, f], from_e.at[g], swap)
+    e2 = [make(mine.at[f, f, :, cells(c)], from_e.at[f, :, cells(c)], swap) for c in pieces]
+    for copy in s[0] + [e1] + s[1] + y:
+        copy.start()
+    loads[0].wait()
+    for k, h in enumerate((g, f)):
+        for c in pieces:
+            s[k][c].wait_recv()
+            near[h, :, cells(c)] += from_s[h, :, cells(c)]
+            x[k][c].start()
+    loads[1].wait()
+    loads[2].wait()
+    for k, h in enumerate((f, g)):
+        y[k].wait_recv()
+        for c in pieces:
+            x[k][c].wait_recv()
+            mine[f, h, :, cells(c)] += from_x[h, :, cells(c)] + from_y[h, :, cells(c)]
+            if k == 0:
+                e2[c].start()
+    e1.wait_recv()
+    mine[f, g] += from_e[f]
+    outgoing = [pltpu.make_async_copy(mine.at[b, g], out.at[b], local.at[i]) for i, b in enumerate((f, g))]
+    outgoing[0].start()
+    for c in pieces:
+        e2[c].wait_recv()
+        mine[g, g, :, cells(c)] += from_e[g, :, cells(c)]
+    outgoing[1].start()
+    for copy in outgoing:
+        copy.wait()
+    for copy in s[0] + s[1] + y + x[0] + x[1] + [e1] + e2:
+        copy.wait_send()
+
+
+def scattered(home, visit):
+    band = pltpu.VMEM((2, HALF, PLANE), jnp.float32)
+    return pl.pallas_call(
+        scatter_kernel,
+        out_shape=jax.ShapeDtypeStruct((2, HALF, PLANE), jnp.float32),
+        in_specs=[HBM, HBM],
+        out_specs=HBM,
+        scratch_shapes=[
+            band, band, band, band, pltpu.VMEM((2, 2, HALF, PLANE), jnp.float32), band,
+            pltpu.SemaphoreType.DMA((18,)), pltpu.SemaphoreType.DMA((18,)), pltpu.SemaphoreType.DMA((3,)),
+        ],
+        compiler_params=pltpu.CompilerParams(collective_id=1, has_side_effects=True, vmem_limit_bytes=60 * 1024 * 1024),
+        name="scatter_terms",
+    )(home, visit)
 
 
 def local(bands):
-    consts = constants()
-    whole = lax.all_gather(bands, "grid", axis=1, tiled=True)
-    share = whole.shape[0] // lax.axis_size("grid")
-    first = lax.axis_index("grid") * share
-    visit = lax.dynamic_slice_in_dim(whole, first, share, 0)
-    visits = jnp.concatenate([shifted(visit, "band", s) for s in (1, 2, 3)], axis=0)
-    home_total, parts = pair_terms(whole, visits, consts)
-    carried = sum(shifted(parts[s : s + 1], "band", -(s + 1)) for s in range(3))
-    own_rows = lax.dynamic_slice_in_dim(home_total, first, share, 0) + carried
-    home_total = lax.dynamic_update_slice_in_dim(home_total, own_rows, first, 0)
-    return sent_and_summed(home_total, "grid", 1)
+    other, visit = gathered(bands)
+    home, parts = pair_terms(bands, other, visit)
+    return scattered(home, parts)
 
 
 def solution(mesh):

time: 331 us -> 177 us (0.53)
  waiting for transfers between devices: 188 us -> 0 us
  Pallas kernels: 48.4 us -> 168 us
  blocking collectives: 37.9 us -> 0 us
  starting transfers between devices: 27.4 us -> 0 us
  between operations: 13.5 us -> 0.03 us
  other arithmetic: 6.81 us -> 0 us
    ppermute x6 -> x0, waiting for transfers between devices: 137 us -> none  [shifted(): return lax.ppermute(value, axis, pairs)]
    pallas_call x1 -> x3, Pallas kernels: 48.4 us -> 168 us  [the longest x1 77.2 us: scattered(): pl.pallas_call(scatter_kernel, out_shape=jax.ShapeDtypeStruct((2, HALF, P...]
    all_gather x1 -> x0, waiting for transfers between devices: 49.8 us -> none  [local(): whole = lax.all_gather(bands, 'grid', axis=1, tiled=True)]
    all_to_all x1 -> x0, blocking collectives: 37.9 us -> none  [sent_and_summed(): lax.all_to_all(split_up(array, dim, devices), axis, 0, 0, tiled=True)]
    ppermute x6 -> x0, starting transfers between devices: 27.4 us -> none  [shifted(): return lax.ppermute(value, axis, pairs)]
    reduce_sum x1 -> x0, other arithmetic: 4.01 us -> none  [sent_and_summed(): return jnp.sum(blocks, axis=0)]
    pallas_call x0 -> x1, local copies, waits for them, and re-layouts: none -> 3.34 us  [scattered(): pl.pallas_call(scatter_kernel, out_shape=jax.ShapeDtypeStruct((2, HALF, P...]
  transfers between devices with their start and end apart: 7 -> 0, of which waited for: 6 -> 0; matrix products, arithmetic and copies ran while one was open for 0% -> 0% of each run, Pallas kernels for 0% -> 0%
where the time goes in v2:
time: 177 us; the launch traced here: 174 us
  Pallas kernels  168 us (95%)
  local copies, waits for them, and re-layouts  6.02 us (3%)
    pallas_call x1, Pallas kernels, scattered(): pl.pallas_call(scatter_kernel, out_shape=jax.ShapeDtypeStruct((2, HALF, P...  77.2 us
    pallas_call x1, Pallas kernels, pair_terms(): pl.pallas_call(pair_kernel, out_shape=(jax.ShapeDtypeStruct((2, 2, HALF,...  48.5 us
    pallas_call x1, Pallas kernels, gathered(): pl.pallas_call(gather_kernel, out_shape=(jax.ShapeDtypeStruct((2, HALF, P...  42.3 us

profile of v2, /device:TPU:4, one launch (start us, length us, event | category | flops | bytes accessed | tf_op | source)
XLA Modules:
  0.0 173.9 jit_solution(17448435522774762008)
XLA Ops:
  0.0 2.7 %copy.9.bands.own = f32[2,36,5184]{2,1,0:T(8,128)} copy(f32[2,36,5184]{2,0,1:T(2,128)} %param.7) | data formatting | bytes 2985984 | tf_op args[0]
  2.7 42.3 %gather_bands.1 = (f32[2,36,5184]{2,1,0:T(8,128)}, f32[3,2,36,5184]{3,2,1,0:T(8,128)}) custom-call(f32[2,36,5184]{2,1,0:T(8,128)} %copy.9.bands.own), custom_call_target="tpu_custom_call" | custom-call | tf_op jit(solution)/shard_map/gather_bands/pallas_call | solution.py:342
  44.9 48.5 %pair_terms.1 = (f32[2,2,36,5184]{3,2,1,0:T(8,128)}, f32[3,2,36,5184]{3,2,1,0:T(8,128)}) custom-call(f32[2,36,5184]{2,1,0:T(8,128)} %copy.9.bands.own, f32[2,36,5184]{2,1,0:T(8,128)} %get-tuple-element.9.other, f32[3,2,36,5184]{3,2,1,0:T(8,128)} %get-tuple-element.10.visit_in, f32[72,216]{1,0:T(8,128)} %constant.12.clone.ahead, ...), custom_call_target="tpu_custom_call" | custom-call | tf_op jit(solution)/shard_map/pair_terms/pallas_call | solution.py:254
  93.4 77.2 %scatter_terms.1 = f32[2,36,5184]{2,1,0:T(8,128)} custom-call(f32[2,2,36,5184]{3,2,1,0:T(8,128)} %get-tuple-element.11.home, f32[3,2,36,5184]{3,2,1,0:T(8,128)} %get-tuple-element.12.visit), custom_call_target="tpu_custom_call" | custom-call | tf_op jit(solution)/shard_map/scatter_terms/pallas_call | solution.py:408
  170.6 3.3 %copy.10 = f32[2,36,5184]{2,0,1:T(2,128)} copy(f32[2,36,5184]{2,1,0:T(8,128)} %scatter_terms.1) | data formatting | bytes 2985984 | tf_op jit(solution)/shard_map/scatter_terms/pallas_call | solution.py:408

commit v3 on v2

--- a/solution.py
+++ b/solution.py
@@ -276,34 +276,46 @@
 
 def places():
     n, g, count = lax.axis_index("band"), lax.axis_index("grid"), lax.axis_size("band")
-    core = lax.rem(n, 2)
+    core, r = lax.rem(n, 2), lax.rem(n, 4)
     swap = (n, 1 - g)
-    x_to, x_from = (lax.rem(n + 2, count), 1 - g), (lax.rem(n + count - 2, count), 1 - g)
+    x_to = (lax.rem(n + 2, count), 1 - g)
+    x_from = (jnp.where(r == 1, n + 1, lax.rem(n + count - 2, count)), 1 - g)
+    r_to = (lax.rem(n + count - 1, count), 1 - g)
     y_to, y_from = (lax.rem(n + 1 + 2 * core, count), g), (lax.rem(n + count - 3 + 2 * core, count), g)
     side = (n + 1 - 2 * core, g)
-    return g, swap, x_to, x_from, y_to, y_from, side
-
-
-def meet(receivers):
+    return g, r, swap, x_to, x_from, r_to, y_to, y_from, side
+
+
+def meet(senders, count):
     barrier = pltpu.get_barrier_semaphore()
-    for device in receivers:
-        pl.semaphore_signal(barrier, inc=1, device_id=device, device_id_type=MESH)
-    pl.semaphore_wait(barrier, len(receivers))
+    for use, device in senders:
+
+        def signal():
+            pl.semaphore_signal(barrier, inc=1, device_id=device, device_id_type=MESH)
+
+        signal() if use is None else pl.when(use)(signal)
+    pl.semaphore_wait(barrier, count)
 
 
 def sender(send, recv):
     index = iter(range(64))
 
-    def make(src, dst, device):
+    def make(src, dst, device, into=None):
         i = next(index)
-        return pltpu.make_async_remote_copy(src, dst, send.at[i], recv.at[i], device_id=device, device_id_type=MESH)
+        j = i if into is None else into
+        copy = pltpu.make_async_remote_copy(src, dst, send.at[i], recv.at[j], device_id=device, device_id_type=MESH)
+        return copy, i
 
     return make
 
 
 def gather_kernel(bands, other, visit, send, recv):
-    g, swap, x_to, x_from, y_to, y_from, side = places()
-    meet([swap, x_from, y_from, side])
+    g, r, swap, x_to, x_from, r_to, y_to, y_from, side = places()
+    sends_x, relays = r != 3, r == 2
+    meet(
+        [(None, swap), (None, x_from), (None, y_from), (None, side)],
+        3 + jnp.where(sends_x, 1, 0) + jnp.where(relays, 1, 0),
+    )
     make = sender(send, recv)
     f = 1 - g
 
@@ -311,31 +323,77 @@
         return pl.ds(*CHUNKS[c])
 
     pieces = range(len(CHUNKS))
-    e1 = [make(bands.at[g, :, cells(c)], other.at[g, :, cells(c)], swap) for c in pieces]
-    x1 = make(bands.at[f], visit.at[0, g], x_to)
-    y1 = make(bands.at[f], visit.at[2, g], y_to)
-    e2 = make(bands.at[f], other.at[f], swap)
-    x2 = [make(other.at[f, :, cells(c)], visit.at[0, f, :, cells(c)], x_to) for c in pieces]
-    y2 = [make(other.at[f, :, cells(c)], visit.at[2, f, :, cells(c)], y_to) for c in pieces]
-    s1 = make(visit.at[0, f], visit.at[1, f], side)
-    s2 = [make(visit.at[0, g, :, cells(c)], visit.at[1, g, :, cells(c)], side) for c in pieces]
-    for copy in e1 + [x1, y1]:
+
+    def many(src, dst, device, into=None):
+        made = [
+            make(src.at[:, cells(c)], dst.at[:, cells(c)], device, None if into is None else into[c]) for c in pieces
+        ]
+        return [copy for copy, _ in made], [i for _, i in made]
+
+    e1, _ = many(bands.at[g], other.at[g], swap)
+    x1, x1_at = make(bands.at[f], visit.at[0, g], x_to)
+    y1, _ = make(bands.at[f], visit.at[2, g], y_to)
+    e2, _ = make(bands.at[f], other.at[f], swap)
+    x2, x2_at = many(other.at[f], visit.at[0, f], x_to)
+    y2, _ = many(other.at[f], visit.at[2, f], y_to)
+    s1, _ = make(visit.at[0, f], visit.at[1, f], side)
+    s2, _ = many(visit.at[0, g], visit.at[1, g], side)
+    r1, _ = make(visit.at[2, g], visit.at[0, g], r_to, x1_at)
+    r2, _ = many(visit.at[2, f], visit.at[0, f], r_to, x2_at)
+    for copy in e1:
         copy.start()
+
+    @pl.when(sends_x)
+    def _():
+        x1.start()
+
+    y1.start()
     for c in pieces:
         e1[c].wait_recv()
-        x2[c].start()
+
+        @pl.when(sends_x)
+        def _():
+            x2[c].start()
+
         y2[c].start()
     e2.start()
+    y1.wait_recv()
+
+    @pl.when(relays)
+    def _():
+        r1.start()
+
+    @pl.when(relays)
+    def _():
+        for c in pieces:
+            y2[c].wait_recv()
+            r2[c].start()
+
     x1.wait_recv()
     s1.start()
     for c in pieces:
         x2[c].wait_recv()
         s2[c].start()
-    y1.wait_recv()
-    for copy in y2 + [e2, s1] + s2:
+
+    @pl.when(r != 2)
+    def _():
+        for c in pieces:
+            y2[c].wait_recv()
+
+    for copy in [e2, s1] + s2:
         copy.wait_recv()
-    for copy in e1 + [x1, y1, e2] + x2 + y2 + [s1] + s2:
+    for copy in e1 + [y1, e2] + y2 + [s1] + s2:
         copy.wait_send()
+
+    @pl.when(sends_x)
+    def _():
+        for copy in [x1] + x2:
+            copy.wait_send()
+
+    @pl.when(relays)
+    def _():
+        for copy in [r1] + r2:
+            copy.wait_send()
 
 
 def gathered(bands):
@@ -347,46 +405,80 @@
         ),
         in_specs=[HBM],
         out_specs=(HBM, HBM),
-        scratch_shapes=[pltpu.SemaphoreType.DMA((16,)), pltpu.SemaphoreType.DMA((16,))],
+        scratch_shapes=[pltpu.SemaphoreType.DMA((20,)), pltpu.SemaphoreType.DMA((20,))],
         compiler_params=pltpu.CompilerParams(collective_id=0, has_side_effects=True),
         name="gather_bands",
     )(bands)
 
 
-def scatter_kernel(home, visit, out, near, from_s, from_x, from_y, mine, from_e, send, recv, local):
-    g, swap, x_to, x_from, y_to, y_from, side = places()
+def scatter_kernel(home, visit, out, near, far, from_s, from_x, from_y, from_r, mine, from_e, send, recv, local):
+    g, r, swap, x_to, x_from, r_to, y_to, y_from, side = places()
+    sent_x, relayed = r != 3, r == 2
     f = 1 - g
     loads = [pltpu.make_async_copy(visit.at[0], near, local.at[0])]
     loads += [pltpu.make_async_copy(home.at[b], mine.at[b], local.at[1 + b]) for b in range(2)]
+    loads += [pltpu.make_async_copy(visit.at[2], far, local.at[3])]
     for copy in loads:
         copy.start()
-    meet([swap, x_to, y_to, side])
+    meet([(None, swap), (sent_x, x_to), (relayed, r_to), (None, y_to), (None, side)], 4)
     make = sender(send, recv)
     pieces = range(len(CHUNKS))
 
     def cells(c):
         return pl.ds(*CHUNKS[c])
 
-    s = [[make(visit.at[1, h, :, cells(c)], from_s.at[h, :, cells(c)], side) for c in pieces] for h in (g, f)]
-    y = [make(visit.at[2, h], from_y.at[h], y_from) for h in (f, g)]
-    x = [[make(near.at[h, :, cells(c)], from_x.at[h, :, cells(c)], x_from) for c in pieces] for h in (g, f)]
-    e1 = make(home.at[g, f], from_e.at[g], swap)
-    e2 = [make(mine.at[f, f, :, cells(c)], from_e.at[f, :, cells(c)], swap) for c in pieces]
-    for copy in s[0] + [e1] + s[1] + y:
+    def many(src, dst, device):
+        return [make(src.at[:, cells(c)], dst.at[:, cells(c)], device)[0] for c in pieces]
+
+    s = [many(visit.at[1, h], from_s.at[h], side) for h in (g, f)]
+    y = [many(far.at[h], from_y.at[h], y_from) for h in (f, g)]
+    x = [many(near.at[h], from_x.at[h], x_from) for h in (g, f)]
+    q = [many(near.at[h], from_r.at[h], x_from) for h in (g, f)]
+    e1, _ = make(home.at[g, f], from_e.at[g], swap)
+    e2 = many(mine.at[f, f], from_e.at[f], swap)
+    for copy in s[0] + [e1] + s[1]:
         copy.start()
+    loads[3].wait()
+
+    @pl.when(r != 2)
+    def _():
+        for copy in y[0] + y[1]:
+            copy.start()
+
     loads[0].wait()
     for k, h in enumerate((g, f)):
         for c in pieces:
             s[k][c].wait_recv()
             near[h, :, cells(c)] += from_s[h, :, cells(c)]
-            x[k][c].start()
+
+            @pl.when(r != 1)
+            def _():
+                x[k][c].start()
+
+            @pl.when(r == 1)
+            def _():
+                q[k][c].start()
+
+    @pl.when(relayed)
+    def _():
+        for k, h in enumerate((f, g)):
+            for c in pieces:
+                q[k][c].wait_recv()
+                far[h, :, cells(c)] += from_r[h, :, cells(c)]
+                y[k][c].start()
+
     loads[1].wait()
     loads[2].wait()
     for k, h in enumerate((f, g)):
-        y[k].wait_recv()
         for c in pieces:
-            x[k][c].wait_recv()
-            mine[f, h, :, cells(c)] += from_x[h, :, cells(c)] + from_y[h, :, cells(c)]
+
+            @pl.when(sent_x)
+            def _():
+                x[k][c].wait_recv()
+                mine[f, h, :, cells(c)] += from_x[h, :, cells(c)]
+
+            y[k][c].wait_recv()
+            mine[f, h, :, cells(c)] += from_y[h, :, cells(c)]
             if k == 0:
                 e2[c].start()
     e1.wait_recv()
@@ -399,8 +491,18 @@
     outgoing[1].start()
     for copy in outgoing:
         copy.wait()
-    for copy in s[0] + s[1] + y + x[0] + x[1] + [e1] + e2:
+    for copy in s[0] + s[1] + y[0] + y[1] + [e1] + e2:
         copy.wait_send()
+
+    @pl.when(r != 1)
+    def _():
+        for copy in x[0] + x[1]:
+            copy.wait_send()
+
+    @pl.when(r == 1)
+    def _():
+        for copy in q[0] + q[1]:
+            copy.wait_send()
 
 
 def scattered(home, visit):
@@ -411,8 +513,8 @@
         in_specs=[HBM, HBM],
         out_specs=HBM,
         scratch_shapes=[
-            band, band, band, band, pltpu.VMEM((2, 2, HALF, PLANE), jnp.float32), band,
-            pltpu.SemaphoreType.DMA((18,)), pltpu.SemaphoreType.DMA((18,)), pltpu.SemaphoreType.DMA((3,)),
+            band, band, band, band, band, band, pltpu.VMEM((2, 2, HALF, PLANE), jnp.float32), band,
+            pltpu.SemaphoreType.DMA((28,)), pltpu.SemaphoreType.DMA((28,)), pltpu.SemaphoreType.DMA((4,)),
         ],
         compiler_params=pltpu.CompilerParams(collective_id=1, has_side_effects=True, vmem_limit_bytes=60 * 1024 * 1024),
         name="scatter_terms",

time: 177 us -> 160 us (0.904); the launches traced: 174 us -> 160 us
  Pallas kernels: 168 us -> 154 us
    pallas_call x1, Pallas kernels: 77.2 us -> 60.5 us  [scattered(): pl.pallas_call(scatter_kernel, out_shape=jax.ShapeDtypeStruct((2, HALF, P...]
    pallas_call x1, Pallas kernels: 42.3 us -> 45 us  [gathered(): pl.pallas_call(gather_kernel, out_shape=(jax.ShapeDtypeStruct((2, HALF, P...]
where the time goes in v3:
time: 160 us
  Pallas kernels  154 us (96%)
  local copies, waits for them, and re-layouts  6.02 us (4%)
    pallas_call x1, Pallas kernels, scattered(): pl.pallas_call(scatter_kernel, out_shape=jax.ShapeDtypeStruct((2, HALF, P...  60.5 us
    pallas_call x1, Pallas kernels, pair_terms(): pl.pallas_call(pair_kernel, out_shape=(jax.ShapeDtypeStruct((2, 2, HALF,...  48.5 us
    pallas_call x1, Pallas kernels, gathered(): pl.pallas_call(gather_kernel, out_shape=(jax.ShapeDtypeStruct((2, HALF, P...  45 us
    pallas_call x1, local copies, waits for them, and re-layouts, scattered(): pl.pallas_call(scatter_kernel, out_shape=jax.ShapeDtypeStruct((2, HALF, P...  3.34 us

profile of v3, /device:TPU:4, one launch (start us, length us, event | category | flops | bytes accessed | tf_op | source)
XLA Modules:
  0.0 160.1 jit_solution(8718338205695232942)
XLA Ops:
  0.0 2.7 %copy.9.bands.own = f32[2,36,5184]{2,1,0:T(8,128)} copy(f32[2,36,5184]{2,0,1:T(2,128)} %param.7) | data formatting | bytes 2985984 | tf_op args[0]
  2.7 45.0 %gather_bands.1 = (f32[2,36,5184]{2,1,0:T(8,128)}, f32[3,2,36,5184]{3,2,1,0:T(8,128)}) custom-call(f32[2,36,5184]{2,1,0:T(8,128)} %copy.9.bands.own), custom_call_target="tpu_custom_call" | custom-call | tf_op jit(solution)/shard_map/gather_bands/pallas_call | solution.py:400
  47.7 48.5 %pair_terms.1 = (f32[2,2,36,5184]{3,2,1,0:T(8,128)}, f32[3,2,36,5184]{3,2,1,0:T(8,128)}) custom-call(f32[2,36,5184]{2,1,0:T(8,128)} %copy.9.bands.own, f32[2,36,5184]{2,1,0:T(8,128)} %get-tuple-element.9.other, f32[3,2,36,5184]{3,2,1,0:T(8,128)} %get-tuple-element.10.visit_in, f32[72,216]{1,0:T(8,128)} %constant.12.clone.ahead, ...), custom_call_target="tpu_custom_call" | custom-call | tf_op jit(solution)/shard_map/pair_terms/pallas_call | solution.py:254
  96.2 60.5 %scatter_terms.1 = f32[2,36,5184]{2,1,0:T(8,128)} custom-call(f32[2,2,36,5184]{3,2,1,0:T(8,128)} %get-tuple-element.11.home, f32[3,2,36,5184]{3,2,1,0:T(8,128)} %get-tuple-element.12.visit), custom_call_target="tpu_custom_call" | custom-call | tf_op jit(solution)/shard_map/scatter_terms/pallas_call | solution.py:510
  156.7 3.3 %copy.10 = f32[2,36,5184]{2,0,1:T(2,128)} copy(f32[2,36,5184]{2,1,0:T(8,128)} %scatter_terms.1) | data formatting | bytes 2985984 | tf_op jit(solution)/shard_map/scatter_terms/pallas_call | solution.py:510

commit v4 on v1

--- a/solution.py
+++ b/solution.py
@@ -14,26 +14,11 @@
 LANES = 128
 ROWS = N * N
 PLANE = N * N
-STEPS = 3
+MESH = pl.DeviceIdType.MESH
+PADDED = 80
+CHUNKS = ((0, 1792), (1792, 1792), (3584, 1600))
 STRIP = 8
 spacing = 0.5167
-
-
-def shifted(value, axis, steps):
-    count = lax.axis_size(axis)
-    pairs = [(source, (source + steps) % count) for source in range(count)]
-    return lax.ppermute(value, axis, pairs)
-
-
-def split_up(array, dim, devices):
-    before, after = (array.shape[:dim], array.shape[dim + 1 :])
-    return jnp.moveaxis(array.reshape(*before, devices, -1, *after), dim, 0)
-
-
-def sent_and_summed(array, axis, dim):
-    devices = lax.axis_size(axis)
-    blocks = lax.all_to_all(split_up(array, dim, devices), axis, 0, 0, tiled=True)
-    return jnp.sum(blocks, axis=0)
 
 
 def rounded(x):
@@ -55,7 +40,10 @@
         wide[N:, LANES : LANES + N] = m
         return np.stack([rounded(wide), rounded(wide - rounded(wide))])
 
-    return stacked(table), stacked(table.T), blocks(table.T), blocks(table.T).transpose(0, 2, 1)
+    halves = np.concatenate([np.arange(HALF), np.arange(HALF) + PADDED // 2])
+    halved = np.zeros((N, PADDED), np.float32)
+    halved[:, halves] = table
+    return stacked(table), stacked(table.T), stacked(halved), stacked(halved.T), blocks(table.T), blocks(table.T).transpose(0, 2, 1)
 
 
 def dot(a, b):
@@ -68,6 +56,11 @@
 
 def down(table, x):
     return dot(table, jnp.concatenate([x, low_part(x), x], axis=0))
+
+
+def joined(x):
+    gap = jnp.zeros((PADDED // 2 - HALF, x[0].shape[1]), jnp.float32)
+    return jnp.concatenate([x[0], gap, x[1], gap], axis=0)
 
 
 def along(x, high, low):
@@ -105,7 +98,8 @@
     lax.fori_loop(0, N, fill, 0)
 
 
-def exchange(homes, visit, home_outs, visit_out, first, ahead, back, lane_ahead, lane_back, factors, u, w):
+def exchange(homes, visit, home_outs, visit_out, first, tables, lane_ahead, lane_back, factors, u, w):
+    ahead, back, half_ahead, half_back = tables
     BODY = 5
     WIDE = 2 * LANES
     TAIL = PLANE // WIDE * WIDE
@@ -113,10 +107,10 @@
     def flat_ahead(tiles):
         for at, width in tiles:
             for p in range(2):
-                x = homes[p][:, pl.ds(at, width)] * visit[:, pl.ds(at, width)]
+                x = joined([homes[p][h, :, pl.ds(at, width)] * visit[h, :, pl.ds(at, width)] for h in range(2)])
                 if width < LANES:
-                    x = jnp.concatenate([x, jnp.zeros((N, LANES - width), jnp.float32)], axis=1)
-                u[p, :, pl.ds(at, max(width, LANES))] = down(ahead[...], x)
+                    x = jnp.concatenate([x, jnp.zeros((PADDED, LANES - width), jnp.float32)], axis=1)
+                u[p, :, pl.ds(at, max(width, LANES))] = down(half_ahead[...], x)
 
     def wide_tiles(i):
         return [(pl.multiple_of((i * BODY + k) * WIDE, LANES), WIDE) for k in range(BODY)]
@@ -205,14 +199,16 @@
     def flat_back(tiles):
         for at, width in tiles:
             cells = pl.ds(at, width)
-            total = None
+            total = [0.0, 0.0]
             for p in range(2):
-                v = down(back[...], u[p, :, pl.ds(at, max(width, LANES))])[:, :width]
-                mine = v * visit[:, cells]
-                home_outs[p][:, cells] = -mine if first else home_outs[p][:, cells] - mine
-                part = v * homes[p][:, cells]
-                total = part if total is None else total + part
-            visit_out[:, cells] = -total
+                v = down(half_back[...], u[p, :, pl.ds(at, max(width, LANES))])[:, :width]
+                for h in range(2):
+                    part = v[PADDED // 2 * h : PADDED // 2 * h + HALF]
+                    mine = part * visit[h, :, cells]
+                    home_outs[p][h, :, cells] = -mine if first else home_outs[p][h, :, cells] - mine
+                    total[h] = total[h] - part * homes[p][h, :, cells]
+            for h in range(2):
+                visit_out[h, :, cells] = total[h]
 
     def pass_5(i, _):
         flat_back(wide_tiles(i))
@@ -222,68 +218,238 @@
     flat_back([(TAIL, PLANE - TAIL)])
 
 
-def kernel(
-    home_in, visit_in, ahead, back, wide_ahead, wide_back, home_out, visit_out,
-    flat, outs, lane_ahead, lane_back, factors, u, w, sems,
+HBM = pl.BlockSpec(memory_space=pl.ANY)
+VMEM = pl.BlockSpec(memory_space=pltpu.VMEM)
+
+
+def places():
+    n, g, count = lax.axis_index("band"), lax.axis_index("grid"), lax.axis_size("band")
+    core, r = lax.rem(n, 2), lax.rem(n, 4)
+    swap = (n, 1 - g)
+    x_to = (lax.rem(n + 2, count), 1 - g)
+    x_from = (jnp.where(r == 1, n + 1, lax.rem(n + count - 2, count)), 1 - g)
+    r_to = (lax.rem(n + count - 1, count), 1 - g)
+    y_to, y_from = (lax.rem(n + 1 + 2 * core, count), g), (lax.rem(n + count - 3 + 2 * core, count), g)
+    side = (n + 1 - 2 * core, g)
+    return g, r, swap, x_to, x_from, r_to, y_to, y_from, side
+
+
+def meet(senders, count):
+    barrier = pltpu.get_barrier_semaphore()
+    for use, device in senders:
+
+        def signal():
+            pl.semaphore_signal(barrier, inc=1, device_id=device, device_id_type=MESH)
+
+        signal() if use is None else pl.when(use)(signal)
+    pl.semaphore_wait(barrier, count)
+
+
+def sender(send, recv):
+    index = iter(range(64))
+
+    def make(src, dst, device, into=None):
+        i = next(index)
+        j = i if into is None else into
+        copy = pltpu.make_async_remote_copy(src, dst, send.at[i], recv.at[j], device_id=device, device_id_type=MESH)
+        return copy, i
+
+    return make
+
+
+def exchange_kernel(
+    bands, ahead, back, half_ahead, half_back, wide_ahead, wide_back, out,
+    flat, outs, lane_ahead, lane_back, factors, u, w, from_s, from_x, from_y, from_r, from_e, send, recv, local,
 ):
-    copies = [pltpu.make_async_copy(home_in.at[i], flat.at[i], sems.at[i]) for i in range(2)]
-    copies += [pltpu.make_async_copy(visit_in.at[i], flat.at[2 + i], sems.at[2 + i]) for i in range(3)]
-    for copy in copies:
+    g, r, swap, x_to, x_from, r_to, y_to, y_from, side = places()
+    sends_x, relays = r != 3, r == 2
+    f = 1 - g
+    pieces = range(len(CHUNKS))
+    make = sender(send, recv)
+
+    def cells(c):
+        return pl.ds(*CHUNKS[c])
+
+    def many(src, dst, device, into=None):
+        made = [
+            make(src.at[:, cells(c)], dst.at[:, cells(c)], device, None if into is None else into[c]) for c in pieces
+        ]
+        return [copy for copy, _ in made], [i for _, i in made]
+
+    meet(
+        [(None, swap), (None, x_from), (None, y_from), (None, side)],
+        3 + jnp.where(sends_x, 1, 0) + jnp.where(relays, 1, 0),
+    )
+    e1, _ = many(bands.at[g], flat.at[g, g], swap)
+    x1, x1_at = make(bands.at[f], flat.at[2, g], x_to)
+    y1, _ = make(bands.at[f], flat.at[4, g], y_to)
+    e2, _ = make(bands.at[f], flat.at[f, g], swap)
+    x2, x2_at = many(flat.at[f, f], flat.at[2, f], x_to)
+    y2, _ = many(flat.at[f, f], flat.at[4, f], y_to)
+    s1, _ = make(flat.at[2, f], flat.at[3, f], side)
+    s2, _ = many(flat.at[2, g], flat.at[3, g], side)
+    r1, _ = make(flat.at[4, g], flat.at[2, g], r_to, x1_at)
+    r2, _ = many(flat.at[4, f], flat.at[2, f], r_to, x2_at)
+    loads = [pltpu.make_async_copy(bands.at[b], flat.at[b, g], local.at[b]) for b in range(2)]
+    for copy in e1:
+        copy.start()
+
+    @pl.when(sends_x)
+    def _():
+        x1.start()
+
+    y1.start()
+    for copy in loads:
         copy.start()
     fill_tables(wide_ahead, wide_back, lane_ahead, lane_back, factors)
-    for copy in copies:
+    for c in pieces:
+        e1[c].wait_recv()
+
+        @pl.when(sends_x)
+        def _():
+            x2[c].start()
+
+        y2[c].start()
+    e2.start()
+    y1.wait_recv()
+
+    @pl.when(relays)
+    def _():
+        r1.start()
+        for c in pieces:
+            y2[c].wait_recv()
+            r2[c].start()
+
+    x1.wait_recv()
+    s1.start()
+    for c in pieces:
+        x2[c].wait_recv()
+        s2[c].start()
+    for copy in loads:
         copy.wait()
-    for j in range(3):
+    e2.wait_recv()
+
+    def pairs(slot, first):
         exchange(
-            [flat.at[0], flat.at[1]], flat.at[2 + j], [outs.at[0], outs.at[1]], outs.at[2 + j], j == 0,
-            ahead, back, lane_ahead, lane_back, factors, u, w,
+            [flat.at[0], flat.at[1]], flat.at[slot], [outs.at[0], outs.at[1]], outs.at[slot], first,
+            (ahead, back, half_ahead, half_back), lane_ahead, lane_back, factors, u, w,
         )
-    copies = [pltpu.make_async_copy(outs.at[i], home_out.at[i], sems.at[i]) for i in range(2)]
-    copies += [pltpu.make_async_copy(outs.at[2 + i], visit_out.at[i], sems.at[2 + i]) for i in range(3)]
-    for copy in copies:
+
+    s_back = [many(outs.at[3, h], from_s.at[h], side)[0] for h in (g, f)]
+    y_back = [many(outs.at[4, h], from_y.at[h], y_from)[0] for h in (f, g)]
+    x_back = [many(outs.at[2, h], from_x.at[h], x_from)[0] for h in (g, f)]
+    r_back = [many(outs.at[2, h], from_r.at[h], x_from)[0] for h in (g, f)]
+    e1_back, _ = make(outs.at[g, f], from_e.at[g], swap)
+    e2_back, _ = many(outs.at[f, f], from_e.at[f], swap)
+
+    pairs(2, True)
+    s1.wait_recv()
+    for copy in s2:
+        copy.wait_recv()
+    pairs(3, False)
+    for copy in s_back[0] + s_back[1]:
         copy.start()
-    for copy in copies:
+    for k, h in enumerate((g, f)):
+        for c in pieces:
+            s_back[k][c].wait_recv()
+            outs[2, h, :, cells(c)] += from_s[h, :, cells(c)]
+
+            @pl.when(r != 1)
+            def _():
+                x_back[k][c].start()
+
+            @pl.when(r == 1)
+            def _():
+                r_back[k][c].start()
+
+    @pl.when(r != 2)
+    def _():
+        for c in pieces:
+            y2[c].wait_recv()
+
+    pairs(4, False)
+    e1_back.start()
+
+    @pl.when(r != 2)
+    def _():
+        for copy in y_back[0] + y_back[1]:
+            copy.start()
+
+    @pl.when(relays)
+    def _():
+        for k, h in enumerate((f, g)):
+            for c in pieces:
+                r_back[k][c].wait_recv()
+                outs[4, h, :, cells(c)] += from_r[h, :, cells(c)]
+                y_back[k][c].start()
+
+    for k, h in enumerate((f, g)):
+        for c in pieces:
+
+            @pl.when(sends_x)
+            def _():
+                x_back[k][c].wait_recv()
+                outs[f, h, :, cells(c)] += from_x[h, :, cells(c)]
+
+            y_back[k][c].wait_recv()
+            outs[f, h, :, cells(c)] += from_y[h, :, cells(c)]
+            if k == 0:
+                e2_back[c].start()
+    e1_back.wait_recv()
+    outs[f, g] += from_e[f]
+    stores = [pltpu.make_async_copy(outs.at[b, g], out.at[b], local.at[i]) for i, b in enumerate((f, g))]
+    stores[0].start()
+    for c in pieces:
+        e2_back[c].wait_recv()
+        outs[g, g, :, cells(c)] += from_e[g, :, cells(c)]
+    stores[1].start()
+    for copy in stores:
         copy.wait()
-
-
-def pair_terms(home, visit, consts):
-    hbm = pl.BlockSpec(memory_space=pl.ANY)
-    vmem = pl.BlockSpec(memory_space=pltpu.VMEM)
+    for copy in e1 + [y1, e2] + y2 + [s1] + s2 + s_back[0] + s_back[1] + y_back[0] + y_back[1] + [e1_back] + e2_back:
+        copy.wait_send()
+
+    @pl.when(sends_x)
+    def _():
+        for copy in [x1] + x2:
+            copy.wait_send()
+
+    @pl.when(relays)
+    def _():
+        for copy in [r1] + r2:
+            copy.wait_send()
+
+    @pl.when(r != 1)
+    def _():
+        for copy in x_back[0] + x_back[1]:
+            copy.wait_send()
+
+    @pl.when(r == 1)
+    def _():
+        for copy in r_back[0] + r_back[1]:
+            copy.wait_send()
+
+
+def local(bands):
+    band = pltpu.VMEM((2, HALF, PLANE), jnp.float32)
+    table = pltpu.VMEM((8, 2, 2 * LANES, 2 * LANES), jnp.float32)
     return pl.pallas_call(
-        kernel,
-        out_shape=(
-            jax.ShapeDtypeStruct((2, N, PLANE), jnp.float32),
-            jax.ShapeDtypeStruct((3, N, PLANE), jnp.float32),
-        ),
-        in_specs=[hbm, hbm, vmem, vmem, vmem, vmem],
-        out_specs=(hbm, hbm),
+        exchange_kernel,
+        out_shape=jax.ShapeDtypeStruct((2, HALF, PLANE), jnp.float32),
+        in_specs=[HBM] + [VMEM] * 6,
+        out_specs=HBM,
         scratch_shapes=[
-            pltpu.VMEM((5, N, PLANE), jnp.float32),
-            pltpu.VMEM((5, N, PLANE), jnp.float32),
-            pltpu.VMEM((8, 2, 2 * LANES, 2 * LANES), jnp.float32),
-            pltpu.VMEM((8, 2, 2 * LANES, 2 * LANES), jnp.float32),
+            pltpu.VMEM((5, 2, HALF, PLANE), jnp.float32),
+            pltpu.VMEM((5, 2, HALF, PLANE), jnp.float32),
+            table, table,
             pltpu.VMEM((ROWS, LANES), jnp.float32),
             pltpu.VMEM((2, N, 41 * LANES), jnp.float32),
             pltpu.VMEM((2, ROWS, LANES), jnp.float32),
-            pltpu.SemaphoreType.DMA((5,)),
+            band, band, band, band, band,
+            pltpu.SemaphoreType.DMA((48,)), pltpu.SemaphoreType.DMA((48,)), pltpu.SemaphoreType.DMA((2,)),
         ],
-        compiler_params=pltpu.CompilerParams(vmem_limit_bytes=60 * 1024 * 1024),
-        name="pair_terms",
-    )(home, visit, *consts)
-
-
-def local(bands):
-    consts = constants()
-    whole = lax.all_gather(bands, "grid", axis=1, tiled=True)
-    share = whole.shape[0] // lax.axis_size("grid")
-    first = lax.axis_index("grid") * share
-    visit = lax.dynamic_slice_in_dim(whole, first, share, 0)
-    visits = jnp.concatenate([shifted(visit, "band", s) for s in (1, 2, 3)], axis=0)
-    home_total, parts = pair_terms(whole, visits, consts)
-    carried = sum(shifted(parts[s : s + 1], "band", -(s + 1)) for s in range(3))
-    own_rows = lax.dynamic_slice_in_dim(home_total, first, share, 0) + carried
-    home_total = lax.dynamic_update_slice_in_dim(home_total, own_rows, first, 0)
-    return sent_and_summed(home_total, "grid", 1)
+        compiler_params=pltpu.CompilerParams(collective_id=0, has_side_effects=True, vmem_limit_bytes=63 * 1024 * 1024),
+        name="exchange_terms",
+    )(bands, *constants())
 
 
 def solution(mesh):

time: 331 us -> 136 us (0.41)
  waiting for transfers between devices: 188 us -> 0 us
  Pallas kernels: 48.4 us -> 127 us
  blocking collectives: 37.9 us -> 0 us
  starting transfers between devices: 27.4 us -> 0 us
  between operations: 13.5 us -> 0.01 us
  other arithmetic: 6.81 us -> 0 us
    ppermute x6 -> x0, waiting for transfers between devices: 137 us -> none  [shifted(): return lax.ppermute(value, axis, pairs)]
    pallas_call x1, Pallas kernels: 48.4 us -> 127 us  [local(): pl.pallas_call(exchange_kernel, out_shape=jax.ShapeDtypeStruct((2, HALF,...]
    all_gather x1 -> x0, waiting for transfers between devices: 49.8 us -> none  [local(): whole = lax.all_gather(bands, 'grid', axis=1, tiled=True)]
    all_to_all x1 -> x0, blocking collectives: 37.9 us -> none  [sent_and_summed(): lax.all_to_all(split_up(array, dim, devices), axis, 0, 0, tiled=True)]
    ppermute x6 -> x0, starting transfers between devices: 27.4 us -> none  [shifted(): return lax.ppermute(value, axis, pairs)]
    reduce_sum x1 -> x0, other arithmetic: 4.01 us -> none  [sent_and_summed(): return jnp.sum(blocks, axis=0)]
    pallas_call x0 -> x1, local copies, waits for them, and re-layouts: none -> 3.34 us  [local(): pl.pallas_call(exchange_kernel, out_shape=jax.ShapeDtypeStruct((2, HALF,...]
  transfers between devices with their start and end apart: 7 -> 0, of which waited for: 6 -> 0; matrix products, arithmetic and copies ran while one was open for 0% -> 0% of each run, Pallas kernels for 0% -> 0%
where the time goes in v4:
time: 136 us; the launch traced here: 133 us
  Pallas kernels  127 us (93%)
  local copies, waits for them, and re-layouts  6.04 us (4%)
    pallas_call x1, Pallas kernels, local(): pl.pallas_call(exchange_kernel, out_shape=jax.ShapeDtypeStruct((2, HALF,...  127 us
    pallas_call x1, local copies, waits for them, and re-layouts, local(): pl.pallas_call(exchange_kernel, out_shape=jax.ShapeDtypeStruct((2, HALF,...  3.34 us

profile of v4, /device:TPU:4, one launch (start us, length us, event | category | flops | bytes accessed | tf_op | source)
XLA Modules:
  0.0 133.3 jit_solution(11392674076353056564)
XLA Ops:
  0.0 2.7 %copy.8.bands = f32[2,36,5184]{2,1,0:T(8,128)} copy(f32[2,36,5184]{2,0,1:T(2,128)} %param.7) | data formatting | bytes 2985984 | tf_op args[0]
  2.7 127.3 %exchange_terms.1 = f32[2,36,5184]{2,1,0:T(8,128)} custom-call(f32[2,36,5184]{2,1,0:T(8,128)} %copy.8.bands, f32[72,216]{1,0:T(8,128)} %constant.12.clone.ahead, f32[72,216]{1,0:T(8,128)} %constant.13.clone.back, f32[72,240]{1,0:T(8,128)} %constant.14.clone.half_ahead, f32[80,216]{1,0:T(8,128)} %constant.15.clone.half_back, ...), custom_call_target="tpu_custom_call" | custom-call | tf_op jit(solution)/shard_map/exchange_terms/pallas_call | solution.py:435
  130.0 3.3 %copy.9 = f32[2,36,5184]{2,0,1:T(2,128)} copy(f32[2,36,5184]{2,1,0:T(8,128)} %exchange_terms.1) | data formatting | bytes 2985984 | tf_op jit(solution)/shard_map/exchange_terms/pallas_call | solution.py:435

commit v5 on v4

--- a/solution.py
+++ b/solution.py
@@ -17,7 +17,7 @@
 MESH = pl.DeviceIdType.MESH
 PADDED = 80
 CHUNKS = ((0, 1792), (1792, 1792), (3584, 1600))
-STRIP = 8
+STRIP = 12
 spacing = 0.5167
 
 
@@ -100,61 +100,72 @@
 
 def exchange(homes, visit, home_outs, visit_out, first, tables, lane_ahead, lane_back, factors, u, w):
     ahead, back, half_ahead, half_back = tables
-    BODY = 5
+    pairs = len(homes)
     WIDE = 2 * LANES
     TAIL = PLANE // WIDE * WIDE
+    body = 20 // pairs
 
     def flat_ahead(tiles):
         for at, width in tiles:
-            for p in range(2):
+            for p in range(pairs):
                 x = joined([homes[p][h, :, pl.ds(at, width)] * visit[h, :, pl.ds(at, width)] for h in range(2)])
                 if width < LANES:
                     x = jnp.concatenate([x, jnp.zeros((PADDED, LANES - width), jnp.float32)], axis=1)
                 u[p, :, pl.ds(at, max(width, LANES))] = down(half_ahead[...], x)
 
     def wide_tiles(i):
-        return [(pl.multiple_of((i * BODY + k) * WIDE, LANES), WIDE) for k in range(BODY)]
-
-    def pass_1(i, _):
-        flat_ahead(wide_tiles(i))
-        return 0
-
-    lax.fori_loop(0, TAIL // WIDE // BODY, pass_1, 0)
+        return [(pl.multiple_of((i * body + k) * WIDE, LANES), WIDE) for k in range(body)]
+
+    def loop(count, work, start=0):
+        def step(i, _):
+            work(i)
+            return 0
+
+        lax.fori_loop(start, count, step, 0)
+
+    loop(TAIL // WIDE // body, lambda i: flat_ahead(wide_tiles(i)))
     flat_ahead([(TAIL, PLANE - TAIL)])
 
-    def lines_ahead(t, count):
-        base = pl.multiple_of(t * 9 * LANES, LANES)
+    def places_of(blocks):
+        return [(p, t) for t in blocks for p in range(pairs)]
+
+    def base(t):
+        return pl.multiple_of(t * 9 * LANES, LANES)
+
+    def line(t, k):
+        return pl.multiple_of((t * 8 + k) * 2 * N, 8)
+
+    def lines_ahead(blocks, count):
         for k in range(count):
             at = 2 * N * k // LANES * LANES
-            x = jnp.concatenate([u[p, :, pl.ds(base + at, WIDE)] for p in range(2)], axis=0)
+            x = jnp.concatenate([u[p, :, pl.ds(base(t) + at, WIDE)] for p, t in places_of(blocks)], axis=0)
             y = along(x, lane_ahead[k, 0], lane_ahead[k, 1])
-            r = pl.multiple_of((t * 8 + k) * 2 * N, 8)
-            for p in range(2):
-                w[p, pl.ds(r, N), :] = y[N * p : N * (p + 1), :LANES]
-                w[p, pl.ds(r + N, N), :] = y[N * p : N * (p + 1), LANES:]
-
-    def pass_2(t, _):
-        lines_ahead(t, 8)
-        return 0
-
-    lax.fori_loop(0, 4, pass_2, 0)
-    lines_ahead(4, 4)
+            for i, (p, t) in enumerate(places_of(blocks)):
+                for half in range(2):
+                    part = y[N * i : N * (i + 1), LANES * half : LANES * (half + 1)]
+                    w[p, pl.ds(line(t, k) + half * N, N), :] = part
+
+    def block_range(i):
+        return [i * 2 // pairs + j for j in range(2 // pairs)]
+
+    loop(2 * pairs, lambda i: lines_ahead(block_range(i), 8))
+    lines_ahead([4], 4)
+
+    def at(i):
+        return [(0, i), (1, i)] if pairs == 2 else [(0, 2 * i), (0, 2 * i + 1)]
 
     def load_w(i):
-        rows = pl.ds(i, N, stride=N)
-        return jnp.concatenate([w[0, rows, :], w[1, rows, :]], axis=1)
+        return jnp.concatenate([w[p, pl.ds(q, N, stride=N), :] for p, q in at(i)], axis=1)
 
     def store_w(i, y):
-        rows = pl.ds(i, N, stride=N)
-        w[0, rows, :] = y[:, :LANES]
-        w[1, rows, :] = y[:, LANES:]
+        for half, (p, q) in enumerate(at(i)):
+            w[p, pl.ds(q, N, stride=N), :] = y[:, LANES * half : LANES * (half + 1)]
 
     def ahead_b(i, x):
         y = down(ahead[...], x)
-        f = factors[pl.ds(pl.multiple_of(i * N, 8), N), :]
-        return y * jnp.concatenate([f, f], axis=1)
-
-    def pass_3(i, _):
+        return y * jnp.concatenate([factors[pl.ds(pl.multiple_of(q * N, 8), N), :] for _, q in at(i)], axis=1)
+
+    def middle(i):
         now = [i * STRIP + k for k in range(STRIP)]
         before = [i * STRIP - STRIP + k for k in range(STRIP)]
         xs, ys = [load_w(q) for q in now], [load_w(q) for q in before]
@@ -164,57 +175,51 @@
             store_w(q, x)
         for q, y in zip(before, ys):
             store_w(q, y)
-        return 0
-
+
+    count = N * pairs // 2
     for q, x in [(q, ahead_b(q, load_w(q))) for q in range(STRIP)]:
         store_w(q, x)
-    lax.fori_loop(1, N // STRIP, pass_3, 0)
-    for q, y in [(q, down(back[...], load_w(q))) for q in range(N - STRIP, N)]:
+    loop(count // STRIP, middle, 1)
+    for q, y in [(q, down(back[...], load_w(q))) for q in range(count - STRIP, count)]:
         store_w(q, y)
 
-    def lines_back(t, count):
-        base = pl.multiple_of(t * 9 * LANES, LANES)
+    def lines_back(blocks, count):
         total = {}
         for k in range(count):
             tile = 2 * N * k // LANES
-            r = pl.multiple_of((t * 8 + k) * 2 * N, 8)
             x = jnp.concatenate(
-                [jnp.concatenate([w[p, pl.ds(r, N), :], w[p, pl.ds(r + N, N), :]], axis=1) for p in range(2)], axis=0
+                [
+                    jnp.concatenate([w[p, pl.ds(line(t, k) + half * N, N), :] for half in range(2)], axis=1)
+                    for p, t in places_of(blocks)
+                ],
+                axis=0,
             )
             y = along(x, lane_back[k, 0], lane_back[k, 1])
             for half in range(2):
                 part = y[:, LANES * half : LANES * (half + 1)]
                 total[tile + half] = total[tile + half] + part if tile + half in total else part
         for tile, value in total.items():
-            for p in range(2):
-                u[p, :, pl.ds(base + tile * LANES, LANES)] = value[N * p : N * (p + 1)]
-
-    def pass_4(t, _):
-        lines_back(t, 8)
-        return 0
-
-    lax.fori_loop(0, 4, pass_4, 0)
-    lines_back(4, 4)
+            for i, (p, t) in enumerate(places_of(blocks)):
+                u[p, :, pl.ds(base(t) + tile * LANES, LANES)] = value[N * i : N * (i + 1)]
+
+    loop(2 * pairs, lambda i: lines_back(block_range(i), 8))
+    lines_back([4], 4)
 
     def flat_back(tiles):
         for at, width in tiles:
             cells = pl.ds(at, width)
-            total = [0.0, 0.0]
-            for p in range(2):
+            total = [0.0 if first[1] else visit_out[h, :, cells] for h in range(2)]
+            for p in range(pairs):
                 v = down(half_back[...], u[p, :, pl.ds(at, max(width, LANES))])[:, :width]
                 for h in range(2):
                     part = v[PADDED // 2 * h : PADDED // 2 * h + HALF]
                     mine = part * visit[h, :, cells]
-                    home_outs[p][h, :, cells] = -mine if first else home_outs[p][h, :, cells] - mine
+                    home_outs[p][h, :, cells] = -mine if first[0] else home_outs[p][h, :, cells] - mine
                     total[h] = total[h] - part * homes[p][h, :, cells]
             for h in range(2):
                 visit_out[h, :, cells] = total[h]
 
-    def pass_5(i, _):
-        flat_back(wide_tiles(i))
-        return 0
-
-    lax.fori_loop(0, TAIL // WIDE // BODY, pass_5, 0)
+    loop(TAIL // WIDE // body, lambda i: flat_back(wide_tiles(i)))
     flat_back([(TAIL, PLANE - TAIL)])
 
 
@@ -311,27 +316,10 @@
 
         y2[c].start()
     e2.start()
-    y1.wait_recv()
-
-    @pl.when(relays)
-    def _():
-        r1.start()
-        for c in pieces:
-            y2[c].wait_recv()
-            r2[c].start()
-
-    x1.wait_recv()
-    s1.start()
-    for c in pieces:
-        x2[c].wait_recv()
-        s2[c].start()
-    for copy in loads:
-        copy.wait()
-    e2.wait_recv()
-
-    def pairs(slot, first):
+
+    def pairs(homes, slot, first):
         exchange(
-            [flat.at[0], flat.at[1]], flat.at[slot], [outs.at[0], outs.at[1]], outs.at[slot], first,
+            [flat.at[b] for b in homes], flat.at[slot], [outs.at[b] for b in homes], outs.at[slot], first,
             (ahead, back, half_ahead, half_back), lane_ahead, lane_back, factors, u, w,
         )
 
@@ -342,13 +330,43 @@
     e1_back, _ = make(outs.at[g, f], from_e.at[g], swap)
     e2_back, _ = many(outs.at[f, f], from_e.at[f], swap)
 
-    pairs(2, True)
+    y1.wait_recv()
+
+    @pl.when(relays)
+    def _():
+        r1.start()
+
+    for c in pieces:
+        y2[c].wait_recv()
+
+        @pl.when(relays)
+        def _():
+            r2[c].start()
+
+    for copy in loads:
+        copy.wait()
+    pairs([f], 4, (True, True))
+    e2.wait_recv()
+    pairs([g], 4, (True, False))
+
+    @pl.when(r != 2)
+    def _():
+        for copy in y_back[0] + y_back[1]:
+            copy.start()
+
+    x1.wait_recv()
+    s1.start()
+    for c in pieces:
+        x2[c].wait_recv()
+        s2[c].start()
+    pairs([0, 1], 2, (False, True))
     s1.wait_recv()
     for copy in s2:
         copy.wait_recv()
-    pairs(3, False)
+    pairs([0, 1], 3, (False, True))
     for copy in s_back[0] + s_back[1]:
         copy.start()
+    e1_back.start()
     for k, h in enumerate((g, f)):
         for c in pieces:
             s_back[k][c].wait_recv()
@@ -361,19 +379,6 @@
             @pl.when(r == 1)
             def _():
                 r_back[k][c].start()
-
-    @pl.when(r != 2)
-    def _():
-        for c in pieces:
-            y2[c].wait_recv()
-
-    pairs(4, False)
-    e1_back.start()
-
-    @pl.when(r != 2)
-    def _():
-        for copy in y_back[0] + y_back[1]:
-            copy.start()
 
     @pl.when(relays)
     def _():

time: 136 us -> 146 us (1.074); the launches traced: 133 us -> 146 us
  Pallas kernels: 127 us -> 140 us
    pallas_call x1, Pallas kernels: 127 us -> 140 us  [local(): pl.pallas_call(exchange_kernel, out_shape=jax.ShapeDtypeStruct((2, HALF,...]
where the time goes in v5:
time: 146 us
  Pallas kernels  140 us (96%)
  local copies, waits for them, and re-layouts  6.04 us (4%)
    pallas_call x1, Pallas kernels, local(): pl.pallas_call(exchange_kernel, out_shape=jax.ShapeDtypeStruct((2, HALF,...  140 us
    pallas_call x1, local copies, waits for them, and re-layouts, local(): pl.pallas_call(exchange_kernel, out_shape=jax.ShapeDtypeStruct((2, HALF,...  3.34 us

profile of v5, /device:TPU:4, one launch (start us, length us, event | category | flops | bytes accessed | tf_op | source)
XLA Modules:
  0.0 145.9 jit_solution(5551490363911870221)
XLA Ops:
  0.0 2.7 %copy.8.bands = f32[2,36,5184]{2,1,0:T(8,128)} copy(f32[2,36,5184]{2,0,1:T(2,128)} %param.7) | data formatting | bytes 2985984 | tf_op args[0]
  2.7 139.8 %exchange_terms.1 = f32[2,36,5184]{2,1,0:T(8,128)} custom-call(f32[2,36,5184]{2,1,0:T(8,128)} %copy.8.bands, f32[72,216]{1,0:T(8,128)} %constant.12.clone.ahead, f32[72,216]{1,0:T(8,128)} %constant.13.clone.back, f32[72,240]{1,0:T(8,128)} %constant.14.clone.half_ahead, f32[80,216]{1,0:T(8,128)} %constant.15.clone.half_back, ...), custom_call_target="tpu_custom_call" | custom-call | tf_op jit(solution)/shard_map/exchange_terms/pallas_call | solution.py:440
  142.5 3.3 %copy.9 = f32[2,36,5184]{2,0,1:T(2,128)} copy(f32[2,36,5184]{2,1,0:T(8,128)} %exchange_terms.1) | data formatting | bytes 2985984 | tf_op jit(solution)/shard_map/exchange_terms/pallas_call | solution.py:440

commit v6 on v5

--- a/solution.py
+++ b/solution.py
@@ -15,8 +15,11 @@
 ROWS = N * N
 PLANE = N * N
 MESH = pl.DeviceIdType.MESH
-PADDED = 80
-CHUNKS = ((0, 1792), (1792, 1792), (3584, 1600))
+LINE = 41 * LANES
+FOLD = 20 * LANES
+LAST = 4 * LINE
+LENGTH = LAST + LINE - FOLD
+CHUNKS = ((0, 62 * LANES), (62 * LANES, 62 * LANES), (124 * LANES, 61 * LANES))
 STRIP = 12
 spacing = 0.5167
 
@@ -40,10 +43,14 @@
         wide[N:, LANES : LANES + N] = m
         return np.stack([rounded(wide), rounded(wide - rounded(wide))])
 
-    halves = np.concatenate([np.arange(HALF), np.arange(HALF) + PADDED // 2])
-    halved = np.zeros((N, PADDED), np.float32)
-    halved[:, halves] = table
-    return stacked(table), stacked(table.T), stacked(halved), stacked(halved.T), blocks(table.T), blocks(table.T).transpose(0, 2, 1)
+    halved = np.zeros((2, N, 80), np.float32)
+    for fold in range(2):
+        for row in range(N):
+            half, r = divmod(row, HALF)
+            halved[fold, :, 40 * half + r + (4 * fold if r >= 32 else 0)] = table[:, row]
+    half_ahead = np.stack([stacked(m) for m in halved])
+    half_back = np.stack([stacked(m.T) for m in halved])
+    return stacked(table), stacked(table.T), half_ahead, half_back, blocks(table.T), blocks(table.T).transpose(0, 2, 1)
 
 
 def dot(a, b):
@@ -58,9 +65,8 @@
     return dot(table, jnp.concatenate([x, low_part(x), x], axis=0))
 
 
-def joined(x):
-    gap = jnp.zeros((PADDED // 2 - HALF, x[0].shape[1]), jnp.float32)
-    return jnp.concatenate([x[0], gap, x[1], gap], axis=0)
+def lanes_of(fold, at, width):
+    return [pl.ds(LINE * i + at, width) for i in range(4)] + [pl.ds(LAST + at - FOLD * fold, width)]
 
 
 def along(x, high, low):
@@ -106,15 +112,16 @@
     body = 20 // pairs
 
     def flat_ahead(tiles):
-        for at, width in tiles:
+        for fold, at, width in tiles:
+            where = lanes_of(fold, at, width)
             for p in range(pairs):
-                x = joined([homes[p][h, :, pl.ds(at, width)] * visit[h, :, pl.ds(at, width)] for h in range(2)])
-                if width < LANES:
-                    x = jnp.concatenate([x, jnp.zeros((PADDED, LANES - width), jnp.float32)], axis=1)
-                u[p, :, pl.ds(at, max(width, LANES))] = down(half_ahead[...], x)
+                x = [homes[p][h, :, lanes] * visit[h, :, lanes] for h in range(2) for lanes in where]
+                u[p, :, pl.ds(at, width)] = down(half_ahead[fold], jnp.concatenate(x, axis=0))
 
     def wide_tiles(i):
-        return [(pl.multiple_of((i * body + k) * WIDE, LANES), WIDE) for k in range(body)]
+        if pairs == 1:
+            return [(k // 10, k * WIDE, WIDE) for k in range(body)]
+        return [(i, pl.multiple_of((i * body + k) * WIDE, LANES), WIDE) for k in range(body)]
 
     def loop(count, work, start=0):
         def step(i, _):
@@ -124,7 +131,7 @@
         lax.fori_loop(start, count, step, 0)
 
     loop(TAIL // WIDE // body, lambda i: flat_ahead(wide_tiles(i)))
-    flat_ahead([(TAIL, PLANE - TAIL)])
+    flat_ahead([(1, TAIL, LANES)])
 
     def places_of(blocks):
         return [(p, t) for t in blocks for p in range(pairs)]
@@ -205,22 +212,28 @@
     loop(2 * pairs, lambda i: lines_back(block_range(i), 8))
     lines_back([4], 4)
 
+    last = pl.ds(LAST, LENGTH - LAST)
+    for out, new in list(zip(home_outs, first[0])) + [(visit_out, first[1])]:
+        if new:
+            for h in range(2):
+                out[h, :, last] = jnp.zeros((8, LENGTH - LAST), jnp.float32)
+
     def flat_back(tiles):
-        for at, width in tiles:
-            cells = pl.ds(at, width)
-            total = [0.0 if first[1] else visit_out[h, :, cells] for h in range(2)]
-            for p in range(pairs):
-                v = down(half_back[...], u[p, :, pl.ds(at, max(width, LANES))])[:, :width]
-                for h in range(2):
-                    part = v[PADDED // 2 * h : PADDED // 2 * h + HALF]
-                    mine = part * visit[h, :, cells]
-                    home_outs[p][h, :, cells] = -mine if first[0] else home_outs[p][h, :, cells] - mine
-                    total[h] = total[h] - part * homes[p][h, :, cells]
+        for fold, at, width in tiles:
+            vs = [down(half_back[fold], u[p, :, pl.ds(at, width)]) for p in range(pairs)]
             for h in range(2):
-                visit_out[h, :, cells] = total[h]
+                for i, lanes in enumerate(lanes_of(fold, at, width)):
+                    total = visit_out[h, :, lanes] if i == 4 or not first[1] else 0.0
+                    other = visit[h, :, lanes]
+                    for p in range(pairs):
+                        part = vs[p][40 * h + 8 * i : 40 * h + 8 * (i + 1)]
+                        before = home_outs[p][h, :, lanes] if i == 4 or not first[0][p] else 0.0
+                        home_outs[p][h, :, lanes] = before - part * other
+                        total = total - part * homes[p][h, :, lanes]
+                    visit_out[h, :, lanes] = total
 
     loop(TAIL // WIDE // body, lambda i: flat_back(wide_tiles(i)))
-    flat_back([(TAIL, PLANE - TAIL)])
+    flat_back([(1, TAIL, LANES)])
 
 
 HBM = pl.BlockSpec(memory_space=pl.ANY)
@@ -345,28 +358,20 @@
 
     for copy in loads:
         copy.wait()
-    pairs([f], 4, (True, True))
+    pairs([f], 4, ((True,), True))
     e2.wait_recv()
-    pairs([g], 4, (True, False))
-
-    @pl.when(r != 2)
-    def _():
-        for copy in y_back[0] + y_back[1]:
-            copy.start()
-
     x1.wait_recv()
     s1.start()
     for c in pieces:
         x2[c].wait_recv()
         s2[c].start()
-    pairs([0, 1], 2, (False, True))
+    pairs([f, g], 2, ((False, True), True))
     s1.wait_recv()
     for copy in s2:
         copy.wait_recv()
-    pairs([0, 1], 3, (False, True))
+    pairs([f, g], 3, ((False, False), True))
     for copy in s_back[0] + s_back[1]:
         copy.start()
-    e1_back.start()
     for k, h in enumerate((g, f)):
         for c in pieces:
             s_back[k][c].wait_recv()
@@ -380,16 +385,22 @@
             def _():
                 r_back[k][c].start()
 
-    @pl.when(relays)
-    def _():
-        for k, h in enumerate((f, g)):
-            for c in pieces:
+    pairs([g], 4, ((False,), False))
+    e1_back.start()
+
+    @pl.when(r != 2)
+    def _():
+        for copy in y_back[0] + y_back[1]:
+            copy.start()
+
+    for k, h in enumerate((f, g)):
+        for c in pieces:
+
+            @pl.when(relays)
+            def _():
                 r_back[k][c].wait_recv()
                 outs[4, h, :, cells(c)] += from_r[h, :, cells(c)]
                 y_back[k][c].start()
-
-    for k, h in enumerate((f, g)):
-        for c in pieces:
 
             @pl.when(sends_x)
             def _():
@@ -434,27 +445,39 @@
             copy.wait_send()
 
 
+def blocked(bands):
+    x = jnp.pad(bands, ((0, 0), (0, 0), (0, LINE - PLANE)))
+    last = jnp.pad(x[:, 32:, :FOLD], ((0, 0), (0, 0), (0, LINE - 2 * FOLD)))
+    parts = [x[:, 8 * i : 8 * (i + 1)] for i in range(4)] + [jnp.concatenate([last, x[:, 32:, FOLD:]], axis=1)]
+    return jnp.concatenate(parts, axis=2)
+
+
+def unblocked(x):
+    last = jnp.concatenate([x[:, :4, LAST : LAST + FOLD], x[:, 4:, LAST : LAST + PLANE - FOLD]], axis=2)
+    return jnp.concatenate([x[:, :, LINE * i : LINE * i + PLANE] for i in range(4)] + [last], axis=1)
+
+
 def local(bands):
-    band = pltpu.VMEM((2, HALF, PLANE), jnp.float32)
+    band = pltpu.VMEM((2, 8, LENGTH), jnp.float32)
+    five = pltpu.VMEM((5, 2, 8, LENGTH), jnp.float32)
     table = pltpu.VMEM((8, 2, 2 * LANES, 2 * LANES), jnp.float32)
-    return pl.pallas_call(
+    terms = pl.pallas_call(
         exchange_kernel,
-        out_shape=jax.ShapeDtypeStruct((2, HALF, PLANE), jnp.float32),
+        out_shape=jax.ShapeDtypeStruct((2, 8, LENGTH), jnp.float32),
         in_specs=[HBM] + [VMEM] * 6,
         out_specs=HBM,
         scratch_shapes=[
-            pltpu.VMEM((5, 2, HALF, PLANE), jnp.float32),
-            pltpu.VMEM((5, 2, HALF, PLANE), jnp.float32),
-            table, table,
+            five, five, table, table,
             pltpu.VMEM((ROWS, LANES), jnp.float32),
-            pltpu.VMEM((2, N, 41 * LANES), jnp.float32),
+            pltpu.VMEM((2, N, LINE), jnp.float32),
             pltpu.VMEM((2, ROWS, LANES), jnp.float32),
             band, band, band, band, band,
             pltpu.SemaphoreType.DMA((48,)), pltpu.SemaphoreType.DMA((48,)), pltpu.SemaphoreType.DMA((2,)),
         ],
         compiler_params=pltpu.CompilerParams(collective_id=0, has_side_effects=True, vmem_limit_bytes=63 * 1024 * 1024),
         name="exchange_terms",
-    )(bands, *constants())
+    )(blocked(bands), *constants())
+    return unblocked(terms)
 
 
 def solution(mesh):

time: 146 us -> 137 us (0.938)
  the two profiles are of different devices: /device:TPU:4 before, /device:TPU:1 now
where the time goes in v6:
time: 137 us
  Pallas kernels  124 us (91%)
  local copies, waits for them, and re-layouts  12.3 us (9%)
    pallas_call x1, Pallas kernels, local(): pl.pallas_call(exchange_kernel, out_shape=jax.ShapeDtypeStruct((2, 8, LEN...  124 us
    unnamed x9, local copies, waits for them, and re-layouts  8.55 us

profile of v6, /device:TPU:1, one launch (start us, length us, event | category | flops | bytes accessed | tf_op | source)
XLA Modules:
  0.0 137.0 jit_solution(12432357599118794187)
XLA Ops:
  0.0 1.5 %copy.8 = f32[2,36,5184]{2,1,0:T(8,128)S(1)} copy(f32[2,36,5184]{2,0,1:T(2,128)} %param.7) | data formatting | bytes 2985984 | tf_op args[0]
  1.5 0.8 fusion
  2.3 0.8 fusion.1
  3.0 0.7 fusion.2
  3.8 0.8 fusion.3
  4.6 0.7 fusion.4.bands
  5.3 123.8 %exchange_terms.1 = f32[2,8,23680]{2,1,0:T(8,128)} custom-call(f32[2,8,23680]{2,1,0:T(8,128)} %fusion.4.bands, f32[72,216]{1,0:T(8,128)} %constant.15.clone.ahead, f32[72,216]{1,0:T(8,128)} %constant.16.clone.back, f32[2,72,240]{2,1,0:T(8,128)} %constant.17.clone.half_ahead, f32[2,80,216]{2,1,0:T(8,128)} %constant.18.clone.half_back, ...), custom_call_target="tpu_custom_call" | custom-call | tf_op jit(solution)/shard_map/exchange_terms/pallas_call | solution.py:464
  129.1 1.0 slice_dynamic-update-slice_fusion.3
  130.1 1.0 slice_dynamic-update-slice_fusion.2
  131.1 1.0 slice_dynamic-update-slice_fusion.1
  132.1 1.0 slice_dynamic-update-slice_fusion
  133.1 0.9 slice.48
  134.1 0.9 slice.47
  135.0 0.1 maximum_dynamic-update-slice_fusion
  135.1 1.9 %copy.10 = f32[2,36,5184]{2,0,1:T(2,128)} copy(f32[2,36,5184]{2,1,0:T(8,128)S(1)} %maximum_dynamic-update-slice_fusion) | data formatting | bytes 2985984 | tf_op jit(solution)/shard_map/concatenate | solution.py:457
  (2 shorter events, 0.0 us)

commit v7 on v6

--- a/solution.py
+++ b/solution.py
@@ -252,7 +252,7 @@
     return g, r, swap, x_to, x_from, r_to, y_to, y_from, side
 
 
-def meet(senders, count):
+def greet(senders):
     barrier = pltpu.get_barrier_semaphore()
     for use, device in senders:
 
@@ -260,7 +260,24 @@
             pl.semaphore_signal(barrier, inc=1, device_id=device, device_id_type=MESH)
 
         signal() if use is None else pl.when(use)(signal)
-    pl.semaphore_wait(barrier, count)
+
+
+def blocked(raw, b, out):
+    for i in range(4):
+        out[:, LINE * i : LINE * i + PLANE] = raw[8 * i : 8 * (i + 1), b, :]
+        out[:, LINE * i + PLANE : LINE * (i + 1)] = jnp.zeros((8, LINE - PLANE), jnp.float32)
+    end = LAST + PLANE - FOLD
+    out[:4, LAST : LAST + FOLD] = raw[32:, b, :FOLD]
+    out[:4, LAST + FOLD :] = jnp.zeros((4, LENGTH - LAST - FOLD), jnp.float32)
+    out[4:, LAST:end] = raw[32:, b, FOLD:]
+    out[4:, end:] = jnp.zeros((4, LENGTH - end), jnp.float32)
+
+
+def unblocked(part, raw, b):
+    for i in range(4):
+        raw[8 * i : 8 * (i + 1), b, :] = part(slice(0, 8), slice(LINE * i, LINE * i + PLANE))
+    raw[32:, b, :FOLD] = part(slice(0, 4), slice(LAST, LAST + FOLD))
+    raw[32:, b, FOLD:] = part(slice(4, 8), slice(LAST, LAST + PLANE - FOLD))
 
 
 def sender(send, recv):
@@ -277,7 +294,7 @@
 
 def exchange_kernel(
     bands, ahead, back, half_ahead, half_back, wide_ahead, wide_back, out,
-    flat, outs, lane_ahead, lane_back, factors, u, w, from_s, from_x, from_y, from_r, from_e, send, recv, local,
+    flat, outs, lane_ahead, lane_back, factors, u, w, from_s, from_x, from_y, from_r, from_e, raw, send, recv, local,
 ):
     g, r, swap, x_to, x_from, r_to, y_to, y_from, side = places()
     sends_x, relays = r != 3, r == 2
@@ -294,21 +311,23 @@
         ]
         return [copy for copy, _ in made], [i for _, i in made]
 
-    meet(
-        [(None, swap), (None, x_from), (None, y_from), (None, side)],
-        3 + jnp.where(sends_x, 1, 0) + jnp.where(relays, 1, 0),
-    )
-    e1, _ = many(bands.at[g], flat.at[g, g], swap)
-    x1, x1_at = make(bands.at[f], flat.at[2, g], x_to)
-    y1, _ = make(bands.at[f], flat.at[4, g], y_to)
-    e2, _ = make(bands.at[f], flat.at[f, g], swap)
+    load = pltpu.make_async_copy(bands, raw, local.at[0])
+    load.start()
+    greet([(None, swap), (None, x_from), (None, y_from), (None, side)])
+    load.wait()
+    for b in range(2):
+        blocked(raw, b, flat.at[b, g])
+    pl.semaphore_wait(pltpu.get_barrier_semaphore(), 3 + jnp.where(sends_x, 1, 0) + jnp.where(relays, 1, 0))
+    e1, _ = many(flat.at[g, g], flat.at[g, g], swap)
+    x1, x1_at = make(flat.at[f, g], flat.at[2, g], x_to)
+    y1, _ = make(flat.at[f, g], flat.at[4, g], y_to)
+    e2, _ = make(flat.at[f, g], flat.at[f, g], swap)
     x2, x2_at = many(flat.at[f, f], flat.at[2, f], x_to)
     y2, _ = many(flat.at[f, f], flat.at[4, f], y_to)
     s1, _ = make(flat.at[2, f], flat.at[3, f], side)
     s2, _ = many(flat.at[2, g], flat.at[3, g], side)
     r1, _ = make(flat.at[4, g], flat.at[2, g], r_to, x1_at)
     r2, _ = many(flat.at[4, f], flat.at[2, f], r_to, x2_at)
-    loads = [pltpu.make_async_copy(bands.at[b], flat.at[b, g], local.at[b]) for b in range(2)]
     for copy in e1:
         copy.start()
 
@@ -317,8 +336,6 @@
         x1.start()
 
     y1.start()
-    for copy in loads:
-        copy.start()
     fill_tables(wide_ahead, wide_back, lane_ahead, lane_back, factors)
     for c in pieces:
         e1[c].wait_recv()
@@ -356,8 +373,6 @@
         def _():
             r2[c].start()
 
-    for copy in loads:
-        copy.wait()
     pairs([f], 4, ((True,), True))
     e2.wait_recv()
     x1.wait_recv()
@@ -411,16 +426,13 @@
             outs[f, h, :, cells(c)] += from_y[h, :, cells(c)]
             if k == 0:
                 e2_back[c].start()
-    e1_back.wait_recv()
-    outs[f, g] += from_e[f]
-    stores = [pltpu.make_async_copy(outs.at[b, g], out.at[b], local.at[i]) for i, b in enumerate((f, g))]
-    stores[0].start()
-    for c in pieces:
-        e2_back[c].wait_recv()
-        outs[g, g, :, cells(c)] += from_e[g, :, cells(c)]
-    stores[1].start()
-    for copy in stores:
-        copy.wait()
+    for copy in [e1_back] + e2_back:
+        copy.wait_recv()
+    for b in range(2):
+        unblocked(lambda rows, lanes: outs[b, g, rows, lanes] + from_e[b, rows, lanes], raw, b)
+    store = pltpu.make_async_copy(raw, out, local.at[0])
+    store.start()
+    store.wait()
     for copy in e1 + [y1, e2] + y2 + [s1] + s2 + s_back[0] + s_back[1] + y_back[0] + y_back[1] + [e1_back] + e2_back:
         copy.wait_send()
 
@@ -443,18 +455,6 @@
     def _():
         for copy in r_back[0] + r_back[1]:
             copy.wait_send()
-
-
-def blocked(bands):
-    x = jnp.pad(bands, ((0, 0), (0, 0), (0, LINE - PLANE)))
-    last = jnp.pad(x[:, 32:, :FOLD], ((0, 0), (0, 0), (0, LINE - 2 * FOLD)))
-    parts = [x[:, 8 * i : 8 * (i + 1)] for i in range(4)] + [jnp.concatenate([last, x[:, 32:, FOLD:]], axis=1)]
-    return jnp.concatenate(parts, axis=2)
-
-
-def unblocked(x):
-    last = jnp.concatenate([x[:, :4, LAST : LAST + FOLD], x[:, 4:, LAST : LAST + PLANE - FOLD]], axis=2)
-    return jnp.concatenate([x[:, :, LINE * i : LINE * i + PLANE] for i in range(4)] + [last], axis=1)
 
 
 def local(bands):
@@ -463,7 +463,7 @@
     table = pltpu.VMEM((8, 2, 2 * LANES, 2 * LANES), jnp.float32)
     terms = pl.pallas_call(
         exchange_kernel,
-        out_shape=jax.ShapeDtypeStruct((2, 8, LENGTH), jnp.float32),
+        out_shape=jax.ShapeDtypeStruct((HALF, 2, PLANE), jnp.float32),
         in_specs=[HBM] + [VMEM] * 6,
         out_specs=HBM,
         scratch_shapes=[
@@ -472,12 +472,13 @@
             pltpu.VMEM((2, N, LINE), jnp.float32),
             pltpu.VMEM((2, ROWS, LANES), jnp.float32),
             band, band, band, band, band,
-            pltpu.SemaphoreType.DMA((48,)), pltpu.SemaphoreType.DMA((48,)), pltpu.SemaphoreType.DMA((2,)),
+            pltpu.VMEM((HALF, 2, PLANE), jnp.float32),
+            pltpu.SemaphoreType.DMA((48,)), pltpu.SemaphoreType.DMA((48,)), pltpu.SemaphoreType.DMA((1,)),
         ],
         compiler_params=pltpu.CompilerParams(collective_id=0, has_side_effects=True, vmem_limit_bytes=63 * 1024 * 1024),
         name="exchange_terms",
-    )(blocked(bands), *constants())
-    return unblocked(terms)
+    )(bands.transpose(1, 0, 2), *constants())
+    return terms.transpose(1, 0, 2)
 
 
 def solution(mesh):

time: 137 us -> 127 us (0.927)
  local copies, waits for them, and re-layouts: 12.3 us -> 2.62 us
    unnamed x9 -> x1, local copies, waits for them, and re-layouts: 8.55 us -> 2.62 us
    concatenate x1 -> x0, local copies, waits for them, and re-layouts: 1.9 us -> none  [unblocked(): jnp.concatenate([x[:, :, LINE * i:LINE * i + PLANE] for i in range(4)] +...]
    slice x4 -> x0, local copies, waits for them, and re-layouts: 1.9 us -> none  [the longest x1 0.94 us: unblocked(): x[:, 4:, LAST:LAST + PLANE - FOLD]]
where the time goes in v7:
time: 127 us
  Pallas kernels  125 us (98%)
  local copies, waits for them, and re-layouts  2.62 us (2%)
    pallas_call x1, Pallas kernels, local(): pl.pallas_call(exchange_kernel, out_shape=jax.ShapeDtypeStruct((HALF, 2,...  125 us
    unnamed x1, local copies, waits for them, and re-layouts  2.62 us

profile of v7, /device:TPU:1, one launch (start us, length us, event | category | flops | bytes accessed | tf_op | source)
XLA Modules:
  0.0 127.2 jit_solution(6771835213816259128)
XLA Ops:
  0.0 124.5 %exchange_terms.1 = f32[36,2,5184]{2,1,0:T(2,128)} custom-call(f32[36,2,5184]{2,1,0:T(2,128)} %bitcast.3, f32[72,216]{1,0:T(8,128)} %constant.12.clone.ahead, f32[72,216]{1,0:T(8,128)} %constant.13.clone.back, f32[2,72,240]{2,1,0:T(8,128)} %constant.14.clone.half_ahead, f32[2,80,216]{2,1,0:T(8,128)} %constant.15.clone.half_back, ...), custom_call_target="tpu_custom_call" | custom-call | tf_op jit(solution)/shard_map/exchange_terms/pallas_call | solution.py:464
  124.6 2.6 %copy.9 = f32[2,36,5184]{2,0,1:T(2,128)} copy(f32[2,36,5184]{2,0,1:T(2,128)} %bitcast.2) | data formatting | bytes 2985984

commit v8 on v7

--- a/solution.py
+++ b/solution.py
@@ -20,7 +20,6 @@
 LAST = 4 * LINE
 LENGTH = LAST + LINE - FOLD
 CHUNKS = ((0, 62 * LANES), (62 * LANES, 62 * LANES), (124 * LANES, 61 * LANES))
-STRIP = 12
 spacing = 0.5167
 
 
@@ -109,7 +108,8 @@
     pairs = len(homes)
     WIDE = 2 * LANES
     TAIL = PLANE // WIDE * WIDE
-    body = 20 // pairs
+    tiles = [(k // 10, k * WIDE, WIDE) for k in range(TAIL // WIDE)] + [(1, TAIL, LANES)]
+    strip = 18 if pairs == 2 else 12
 
     def flat_ahead(tiles):
         for fold, at, width in tiles:
@@ -118,11 +118,6 @@
                 x = [homes[p][h, :, lanes] * visit[h, :, lanes] for h in range(2) for lanes in where]
                 u[p, :, pl.ds(at, width)] = down(half_ahead[fold], jnp.concatenate(x, axis=0))
 
-    def wide_tiles(i):
-        if pairs == 1:
-            return [(k // 10, k * WIDE, WIDE) for k in range(body)]
-        return [(i, pl.multiple_of((i * body + k) * WIDE, LANES), WIDE) for k in range(body)]
-
     def loop(count, work, start=0):
         def step(i, _):
             work(i)
@@ -130,8 +125,7 @@
 
         lax.fori_loop(start, count, step, 0)
 
-    loop(TAIL // WIDE // body, lambda i: flat_ahead(wide_tiles(i)))
-    flat_ahead([(1, TAIL, LANES)])
+    flat_ahead(tiles)
 
     def places_of(blocks):
         return [(p, t) for t in blocks for p in range(pairs)]
@@ -153,9 +147,9 @@
                     w[p, pl.ds(line(t, k) + half * N, N), :] = part
 
     def block_range(i):
-        return [i * 2 // pairs + j for j in range(2 // pairs)]
-
-    loop(2 * pairs, lambda i: lines_ahead(block_range(i), 8))
+        return [i * 4 // pairs + j for j in range(4 // pairs)]
+
+    loop(pairs, lambda i: lines_ahead(block_range(i), 8))
     lines_ahead([4], 4)
 
     def at(i):
@@ -173,8 +167,8 @@
         return y * jnp.concatenate([factors[pl.ds(pl.multiple_of(q * N, 8), N), :] for _, q in at(i)], axis=1)
 
     def middle(i):
-        now = [i * STRIP + k for k in range(STRIP)]
-        before = [i * STRIP - STRIP + k for k in range(STRIP)]
+        now = [i * strip + k for k in range(strip)]
+        before = [i * strip - strip + k for k in range(strip)]
         xs, ys = [load_w(q) for q in now], [load_w(q) for q in before]
         xs = [ahead_b(q, x) for q, x in zip(now, xs)]
         ys = [down(back[...], y) for y in ys]
@@ -184,10 +178,10 @@
             store_w(q, y)
 
     count = N * pairs // 2
-    for q, x in [(q, ahead_b(q, load_w(q))) for q in range(STRIP)]:
+    for q, x in [(q, ahead_b(q, load_w(q))) for q in range(strip)]:
         store_w(q, x)
-    loop(count // STRIP, middle, 1)
-    for q, y in [(q, down(back[...], load_w(q))) for q in range(count - STRIP, count)]:
+    loop(count // strip, middle, 1)
+    for q, y in [(q, down(back[...], load_w(q))) for q in range(count - strip, count)]:
         store_w(q, y)
 
     def lines_back(blocks, count):
@@ -209,7 +203,7 @@
             for i, (p, t) in enumerate(places_of(blocks)):
                 u[p, :, pl.ds(base(t) + tile * LANES, LANES)] = value[N * i : N * (i + 1)]
 
-    loop(2 * pairs, lambda i: lines_back(block_range(i), 8))
+    loop(pairs, lambda i: lines_back(block_range(i), 8))
     lines_back([4], 4)
 
     last = pl.ds(LAST, LENGTH - LAST)
@@ -232,8 +226,7 @@
                         total = total - part * homes[p][h, :, lanes]
                     visit_out[h, :, lanes] = total
 
-    loop(TAIL // WIDE // body, lambda i: flat_back(wide_tiles(i)))
-    flat_back([(1, TAIL, LANES)])
+    flat_back(tiles)
 
 
 HBM = pl.BlockSpec(memory_space=pl.ANY)
@@ -373,20 +366,42 @@
         def _():
             r2[c].start()
 
-    pairs([f], 4, ((True,), True))
-    e2.wait_recv()
+    outs[4] = jnp.zeros((2, 8, LENGTH), jnp.float32)
+
+    def with_y(i, _):
+        @pl.when(i == 1)
+        def _():
+            e2.wait_recv()
+
+        pairs([lax.rem(f + i, 2)], 4, ((True,), False))
+        return 0
+
+    lax.fori_loop(0, 2, with_y, 0)
+
+    @pl.when(r != 2)
+    def _():
+        for copy in y_back[0] + y_back[1]:
+            copy.start()
+
     x1.wait_recv()
     s1.start()
     for c in pieces:
         x2[c].wait_recv()
         s2[c].start()
-    pairs([f, g], 2, ((False, True), True))
-    s1.wait_recv()
-    for copy in s2:
-        copy.wait_recv()
-    pairs([f, g], 3, ((False, False), True))
+
+    def with_x_and_s(i, _):
+        @pl.when(i == 1)
+        def _():
+            for copy in [s1] + s2:
+                copy.wait_recv()
+
+        pairs([0, 1], 2 + i, ((False, False), True))
+        return 0
+
+    lax.fori_loop(0, 2, with_x_and_s, 0)
     for copy in s_back[0] + s_back[1]:
         copy.start()
+    e1_back.start()
     for k, h in enumerate((g, f)):
         for c in pieces:
             s_back[k][c].wait_recv()
@@ -399,14 +414,6 @@
             @pl.when(r == 1)
             def _():
                 r_back[k][c].start()
-
-    pairs([g], 4, ((False,), False))
-    e1_back.start()
-
-    @pl.when(r != 2)
-    def _():
-        for copy in y_back[0] + y_back[1]:
-            copy.start()
 
     for k, h in enumerate((f, g)):
         for c in pieces:

time: 127 us -> 123 us (0.969)
  the two profiles are of different devices: /device:TPU:1 before, /device:TPU:4 now
where the time goes in v8:
time: 123 us; the launch traced here: 121 us
  Pallas kernels  119 us (97%)
  local copies, waits for them, and re-layouts  2.62 us (2%)
    pallas_call x1, Pallas kernels, local(): pl.pallas_call(exchange_kernel, out_shape=jax.ShapeDtypeStruct((HALF, 2,...  119 us
    unnamed x1, local copies, waits for them, and re-layouts  2.62 us

profile of v8, /device:TPU:4, one launch (start us, length us, event | category | flops | bytes accessed | tf_op | source)
XLA Modules:
  0.0 121.3 jit_solution(18298324119252350757)
XLA Ops:
  0.0 118.7 %exchange_terms.1 = f32[36,2,5184]{2,1,0:T(2,128)} custom-call(f32[36,2,5184]{2,1,0:T(2,128)} %bitcast.3, f32[72,216]{1,0:T(8,128)} %constant.12.clone.ahead, f32[72,216]{1,0:T(8,128)} %constant.13.clone.back, f32[2,72,240]{2,1,0:T(8,128)} %constant.14.clone.half_ahead, f32[2,80,216]{2,1,0:T(8,128)} %constant.15.clone.half_back, ...), custom_call_target="tpu_custom_call" | custom-call | tf_op jit(solution)/shard_map/exchange_terms/pallas_call | solution.py:471
  118.7 2.6 %copy.9 = f32[2,36,5184]{2,0,1:T(2,128)} copy(f32[2,36,5184]{2,0,1:T(2,128)} %bitcast.2) | data formatting | bytes 2985984

commit v9 on v8

--- a/solution.py
+++ b/solution.py
@@ -19,7 +19,7 @@
 FOLD = 20 * LANES
 LAST = 4 * LINE
 LENGTH = LAST + LINE - FOLD
-CHUNKS = ((0, 62 * LANES), (62 * LANES, 62 * LANES), (124 * LANES, 61 * LANES))
+CHUNKS = ((0, 46 * LANES), (46 * LANES, 46 * LANES), (92 * LANES, 46 * LANES), (138 * LANES, 47 * LANES))
 spacing = 0.5167
 
 
@@ -147,9 +147,9 @@
                     w[p, pl.ds(line(t, k) + half * N, N), :] = part
 
     def block_range(i):
-        return [i * 4 // pairs + j for j in range(4 // pairs)]
-
-    loop(pairs, lambda i: lines_ahead(block_range(i), 8))
+        return list(range(4))
+
+    loop(1, lambda i: lines_ahead(block_range(i), 8))
     lines_ahead([4], 4)
 
     def at(i):
@@ -203,7 +203,7 @@
             for i, (p, t) in enumerate(places_of(blocks)):
                 u[p, :, pl.ds(base(t) + tile * LANES, LANES)] = value[N * i : N * (i + 1)]
 
-    loop(pairs, lambda i: lines_back(block_range(i), 8))
+    loop(1, lambda i: lines_back(block_range(i), 8))
     lines_back([4], 4)
 
     last = pl.ds(LAST, LENGTH - LAST)
@@ -480,7 +480,7 @@
             pltpu.VMEM((2, ROWS, LANES), jnp.float32),
             band, band, band, band, band,
             pltpu.VMEM((HALF, 2, PLANE), jnp.float32),
-            pltpu.SemaphoreType.DMA((48,)), pltpu.SemaphoreType.DMA((48,)), pltpu.SemaphoreType.DMA((1,)),
+            pltpu.SemaphoreType.DMA((64,)), pltpu.SemaphoreType.DMA((64,)), pltpu.SemaphoreType.DMA((1,)),
         ],
         compiler_params=pltpu.CompilerParams(collective_id=0, has_side_effects=True, vmem_limit_bytes=63 * 1024 * 1024),
         name="exchange_terms",

time: 123 us -> 120 us (0.976)
  Pallas kernels: 119 us -> 116 us
    pallas_call x1, Pallas kernels: 119 us -> 116 us  [local(): pl.pallas_call(exchange_kernel, out_shape=jax.ShapeDtypeStruct((HALF, 2,...]
where the time goes in v9:
time: 120 us; the launch traced here: 119 us
  Pallas kernels  116 us (97%)
  local copies, waits for them, and re-layouts  2.62 us (2%)
    pallas_call x1, Pallas kernels, local(): pl.pallas_call(exchange_kernel, out_shape=jax.ShapeDtypeStruct((HALF, 2,...  116 us
    unnamed x1, local copies, waits for them, and re-layouts  2.62 us

profile of v9, /device:TPU:4, one launch (start us, length us, event | category | flops | bytes accessed | tf_op | source)
XLA Modules:
  0.0 118.6 jit_solution(14130112345951555966)
XLA Ops:
  0.0 116.0 %exchange_terms.1 = f32[36,2,5184]{2,1,0:T(2,128)} custom-call(f32[36,2,5184]{2,1,0:T(2,128)} %bitcast.3, f32[72,216]{1,0:T(8,128)} %constant.12.clone.ahead, f32[72,216]{1,0:T(8,128)} %constant.13.clone.back, f32[2,72,240]{2,1,0:T(8,128)} %constant.14.clone.half_ahead, f32[2,80,216]{2,1,0:T(8,128)} %constant.15.clone.half_back, ...), custom_call_target="tpu_custom_call" | custom-call | tf_op jit(solution)/shard_map/exchange_terms/pallas_call | solution.py:471
  116.0 2.6 %copy.9 = f32[2,36,5184]{2,0,1:T(2,128)} copy(f32[2,36,5184]{2,0,1:T(2,128)} %bitcast.2) | data formatting | bytes 2985984

commit v10 on v9

--- a/solution.py
+++ b/solution.py
@@ -131,26 +131,23 @@
         return [(p, t) for t in blocks for p in range(pairs)]
 
     def base(t):
-        return pl.multiple_of(t * 9 * LANES, LANES)
+        return t * 9 * LANES
 
     def line(t, k):
-        return pl.multiple_of((t * 8 + k) * 2 * N, 8)
-
-    def lines_ahead(blocks, count):
-        for k in range(count):
-            at = 2 * N * k // LANES * LANES
-            x = jnp.concatenate([u[p, :, pl.ds(base(t) + at, WIDE)] for p, t in places_of(blocks)], axis=0)
-            y = along(x, lane_ahead[k, 0], lane_ahead[k, 1])
-            for i, (p, t) in enumerate(places_of(blocks)):
-                for half in range(2):
-                    part = y[N * i : N * (i + 1), LANES * half : LANES * (half + 1)]
-                    w[p, pl.ds(line(t, k) + half * N, N), :] = part
-
-    def block_range(i):
-        return list(range(4))
-
-    loop(1, lambda i: lines_ahead(block_range(i), 8))
-    lines_ahead([4], 4)
+        return (t * 8 + k) * 2 * N
+
+    def blocks_with(k):
+        return range(5) if k < 4 else range(4)
+
+    for k in range(8):
+        at = 2 * N * k // LANES * LANES
+        where = places_of(blocks_with(k))
+        x = jnp.concatenate([u[p, :, pl.ds(base(t) + at, WIDE)] for p, t in where], axis=0)
+        y = along(x, lane_ahead[k, 0], lane_ahead[k, 1])
+        for i, (p, t) in enumerate(where):
+            for half in range(2):
+                part = y[N * i : N * (i + 1), LANES * half : LANES * (half + 1)]
+                w[p, pl.ds(line(t, k) + half * N, N), :] = part
 
     def at(i):
         return [(0, i), (1, i)] if pairs == 2 else [(0, 2 * i), (0, 2 * i + 1)]
@@ -184,27 +181,24 @@
     for q, y in [(q, down(back[...], load_w(q))) for q in range(count - strip, count)]:
         store_w(q, y)
 
-    def lines_back(blocks, count):
-        total = {}
-        for k in range(count):
-            tile = 2 * N * k // LANES
-            x = jnp.concatenate(
-                [
-                    jnp.concatenate([w[p, pl.ds(line(t, k) + half * N, N), :] for half in range(2)], axis=1)
-                    for p, t in places_of(blocks)
-                ],
-                axis=0,
-            )
-            y = along(x, lane_back[k, 0], lane_back[k, 1])
+    total = {}
+    for k in range(8):
+        where = places_of(blocks_with(k))
+        x = jnp.concatenate(
+            [
+                jnp.concatenate([w[p, pl.ds(line(t, k) + half * N, N), :] for half in range(2)], axis=1)
+                for p, t in where
+            ],
+            axis=0,
+        )
+        y = along(x, lane_back[k, 0], lane_back[k, 1])
+        for i, (p, t) in enumerate(where):
             for half in range(2):
-                part = y[:, LANES * half : LANES * (half + 1)]
-                total[tile + half] = total[tile + half] + part if tile + half in total else part
-        for tile, value in total.items():
-            for i, (p, t) in enumerate(places_of(blocks)):
-                u[p, :, pl.ds(base(t) + tile * LANES, LANES)] = value[N * i : N * (i + 1)]
-
-    loop(1, lambda i: lines_back(block_range(i), 8))
-    lines_back([4], 4)
+                part = y[N * i : N * (i + 1), LANES * half : LANES * (half + 1)]
+                key = (p, 9 * t + 2 * N * k // LANES + half)
+                total[key] = total[key] + part if key in total else part
+    for (p, tile), value in total.items():
+        u[p, :, LANES * tile : LANES * (tile + 1)] = value
 
     last = pl.ds(LAST, LENGTH - LAST)
     for out, new in list(zip(home_outs, first[0])) + [(visit_out, first[1])]:

time: 120 us -> 120 us (level)
  no operation moved by 1% of the time
where the time goes in v10:
time: 120 us; the launch traced here: 118 us
  Pallas kernels  116 us (97%)
  local copies, waits for them, and re-layouts  2.62 us (2%)
    pallas_call x1, Pallas kernels, local(): pl.pallas_call(exchange_kernel, out_shape=jax.ShapeDtypeStruct((HALF, 2,...  116 us
    unnamed x1, local copies, waits for them, and re-layouts  2.62 us

profile of v10, /device:TPU:4, one launch (start us, length us, event | category | flops | bytes accessed | tf_op | source)
XLA Modules:
  0.0 118.3 jit_solution(12792261048056428787)
XLA Ops:
  0.0 115.7 %exchange_terms.1 = f32[36,2,5184]{2,1,0:T(2,128)} custom-call(f32[36,2,5184]{2,1,0:T(2,128)} %bitcast.3, f32[72,216]{1,0:T(8,128)} %constant.12.clone.ahead, f32[72,216]{1,0:T(8,128)} %constant.13.clone.back, f32[2,72,240]{2,1,0:T(8,128)} %constant.14.clone.half_ahead, f32[2,80,216]{2,1,0:T(8,128)} %constant.15.clone.half_back, ...), custom_call_target="tpu_custom_call" | custom-call | tf_op jit(solution)/shard_map/exchange_terms/pallas_call | solution.py:465
  115.7 2.6 %copy.9 = f32[2,36,5184]{2,0,1:T(2,128)} copy(f32[2,36,5184]{2,0,1:T(2,128)} %bitcast.2) | data formatting | bytes 2985984
